TPU v7x, 128 devices: a whole 4x4x4 slice. The times are simulated.
128 devices in a mesh: dz: 4 (over z), dy: 4 (over y), dx: 8 (over x, core).
Axes of the slice: x: 4, y: 4, z: 4, core: 2. Of those that a mesh axis runs over, the one named last changes fastest.
Arguments:
- g_emb: float32 [128, 2048, 256], P(('dz', 'dy', 'dx'))
- g_attn: float32 [128, 3, 4, 256, 256], P(('dz', 'dy', 'dx'))
- g_in: float32 [128, 3, 256, 1024], P(('dz', 'dy', 'dx'))
- g_out: float32 [128, 3, 1024, 256], P(('dz', 'dy', 'dx'))
- g_vecd: float32 [128, 3, 9, 256], P(('dz', 'dy', 'dx'))
- g_vecf: float32 [128, 3, 1024], P(('dz', 'dy', 'dx'))
- opt_m: float32 [2899968], P(('dz', 'dy', 'dx'))
- opt_v: float32 [2899968], P(('dz', 'dy', 'dx'))
- master: float32 [2899968], P(('dz', 'dy', 'dx'))
- tok_ids: int32 [32768], P(('dz', 'dy', 'dx'))
- act_in: bfloat16 [32768, 256], P(('dz', 'dy', 'dx'))
Outputs:
- output 1: float32 [2899968], P(('dz', 'dy', 'dx'))
- output 2: float32 [2899968], P(('dz', 'dy', 'dx'))
- output 3: float32 [2899968], P(('dz', 'dy', 'dx'))
- output 4: bfloat16 [2048, 256], replicated
- output 5: bfloat16 [3, 4, 256, 256], replicated
- output 6: bfloat16 [3, 256, 1024], replicated
- output 7: bfloat16 [3, 1024, 256], replicated
- output 8: bfloat16 [3, 9, 256], replicated
- output 9: bfloat16 [3, 1024], replicated
- output 10: bfloat16 [32768, 256], P(('dz', 'dy', 'dx'))
All inputs are finite; a program needn't handle non-finite values.
Results may differ from a plain program's by a relative error of at most 0.001.
Values are sent between devices in bfloat16 or wider.
A program may use at most 1 GiB of HBM per device.

v0:
```python
import math
import jax
import jax.numpy as jnp
from jax import lax
from jax.sharding import PartitionSpec as P

LEARN_RATE = 0.002
BETA_ONE = 0.9
BETA_TWO = 0.95
ADAM_EPS = 1e-8
ADAM_STEP = 2
AXES = ("dz", "dy", "dx")
GRAD_RANKS = (3, 5, 4, 4, 4, 3)


def adam_update(grad_vals, opt_m, opt_v, master):
    m_new = BETA_ONE * opt_m + (1.0 - BETA_ONE) * grad_vals
    v_new = BETA_TWO * opt_v + (1.0 - BETA_TWO) * grad_vals * grad_vals
    m_hat = m_new / (1.0 - BETA_ONE ** ADAM_STEP)
    v_hat = v_new / (1.0 - BETA_TWO ** ADAM_STEP)
    w_new = master - LEARN_RATE * m_hat / (jnp.sqrt(v_hat) + ADAM_EPS)
    return m_new, v_new, w_new


def split_flat(flat_vals, shapes):
    pieces = []
    offset = 0
    for tensor_shape in shapes:
        elem_count = math.prod(tensor_shape)
        pieces.append(flat_vals[offset:offset + elem_count].reshape(tensor_shape))
        offset = offset + elem_count
    return pieces


def ffn_block(wb_emb, w_in, b_in, w_out, b_out, tok_ids, act_in):
    emb_rows = jnp.take(wb_emb, tok_ids, axis=0).astype(jnp.float32)
    hidden = (emb_rows * math.sqrt(wb_emb.shape[1]) + act_in.astype(jnp.float32)).astype(jnp.bfloat16)
    pre_act = jnp.dot(hidden, w_in, preferred_element_type=jnp.float32) + b_in.astype(jnp.float32)
    inner_act = jax.nn.gelu(pre_act, approximate=True).astype(jnp.bfloat16)
    return (jnp.dot(inner_act, w_out, preferred_element_type=jnp.float32) + b_out.astype(jnp.float32)).astype(jnp.bfloat16)


def solution(mesh):
    devices = math.prod([mesh.shape[axis_name] for axis_name in AXES])

    def device_step(g_emb, g_attn, g_in, g_out, g_vecd, g_vecf, opt_m, opt_v, master, tok_ids, act_in):
        grad_list = [g_emb, g_attn, g_in, g_out, g_vecd, g_vecf]
        shapes = [grad_arr.shape[1:] for grad_arr in grad_list]
        param_count = sum(math.prod(tensor_shape) for tensor_shape in shapes)
        shard_len = opt_m.shape[0]
        local_flat = jnp.concatenate([grad_arr.reshape(-1) for grad_arr in grad_list])
        local_flat = jnp.pad(local_flat, (0, shard_len * devices - param_count))
        grad_shard = lax.psum_scatter(local_flat, AXES, scatter_dimension=0, tiled=True) / devices
        m_new, v_new, w_new = adam_update(grad_shard, opt_m, opt_v, master)
        full_half = lax.all_gather(w_new.astype(jnp.bfloat16), AXES, axis=0, tiled=True)
        wb_emb, wb_attn, wb_in, wb_out, wb_vecd, wb_vecf = split_flat(full_half, shapes)
        y_out = ffn_block(wb_emb, wb_in[0], wb_vecf[0], wb_out[0], wb_vecd[0, 8], tok_ids, act_in)
        return (m_new, v_new, w_new, wb_emb, wb_attn, wb_in, wb_out, wb_vecd, wb_vecf, y_out)

    grad_specs = tuple(P(AXES, *([None] * (grad_rank - 1))) for grad_rank in GRAD_RANKS)
    in_specs = grad_specs + (P(AXES), P(AXES), P(AXES), P(AXES), P(AXES, None))
    out_specs = (P(AXES), P(AXES), P(AXES), P(), P(), P(), P(), P(), P(), P(AXES, None))
    return jax.shard_map(device_step, mesh=mesh, in_specs=in_specs, out_specs=out_specs, check_vma=False)
```

profile of v0, /device:TPU:1, one launch (start us, length us, event | category | flops | bytes accessed | tf_op | source)
XLA Modules:
  0.0 364.5 jit_solution(14289593844367340914)
XLA Ops:
  7.2 2.8 copy.23
  10.1 1.6 constant_dynamic-update-slice_fusion.5
  11.7 3.3 copy.24
  14.9 2.4 copy.25
  17.4 1.6 copy.26
  19.1 3.9 %constant_dynamic-update-slice_fusion.4 = f32[2893568]{0:T(1024)} fusion(f32[2893568]{0:T(1024)} %constant_dynamic-update-slice_fusion.5, f32[786432]{0:T(1024)} %bitcast.14), kind=kLoop, calls=%fused_computation.31 | loop fusion | bytes 6291456
  23.0 1.9 constant_dynamic-update-slice_fusion.3
  24.8 1.9 constant_dynamic-update-slice_fusion.2
  26.7 1.4 constant_dynamic-update-slice_fusion.1
  28.1 1.3 constant_dynamic-update-slice_fusion
  29.4 10.0 %pad.4 = f32[2899968]{0:T(1024)} pad(f32[2893568]{0:T(1024)} %constant_dynamic-update-slice_fusion, f32[]{:T(128)} %constant.19.clone.1), padding=0_6400 | pad | bytes 23174148 | tf_op jit(solution)/shard_map/jit(_pad)/pad | solution.py:52
  39.5 0.2 all-gather.3.cloned.1.call-start
  39.7 169.0 %all-reduce.4.cloned.1.call-done = f32[2899968]{0:T(1024)} async-done(((f32[2899968]{0:T(1024)}), f32[2899968]{0:T(1024)}) %all-reduce.4.cloned.1.call-update) | async-done | bytes 11599888
  208.7 1.7 fusion.30
  210.4 0.7 reshape.124
  211.2 72.0 %all-gather.3.cloned.1.call-done = bf16[128,1,22656]{2,1,0:T(2,128)(2,1)} async-done(((bf16[1,1,22656]{2,1,0:T(2,128)(2,1)}), bf16[128,1,22656]{2,1,0:T(2,128)(2,1)}) %all-gather.3.cloned.1.call-update) | async-done | bytes 5799952 | tf_op jit(solution)/shard_map/all_gather | solution.py:55
  283.2 36.4 %reduce.1 = bf16[128,22656]{1,0:T(8,128)(2,1)} reduce(bf16[128,1,22656]{2,1,0:T(2,128)(2,1)} %all-gather.3.cloned.1.call-done, bf16[]{:T(256)} %constant.64), dimensions={1}, to_apply=%all-gather.reduce_sub_computation | reduce | bytes 11599874 | tf_op jit(solution)/shard_map/all_gather | solution.py:55
  319.6 11.8 %reshape.125 = bf16[2899968]{0:T(1024)(128)(2,1)} reshape(bf16[128,22656]{1,0:T(8,128)(2,1)} %reduce.1) | data formatting | bytes 11599872
  331.4 2.1 fusion.31
  333.6 0.7 slice_convert_fusion
  334.2 4.3 %fusion.32 = (bf16[786432]{0:T(1024)(128)(2,1)S(1)}, bf16[786432]{0:T(1024)(128)(2,1)}, bf16[786432]{0:T(1024)(128)(2,1)}) fusion(bf16[2899968]{0:T(1024)(128)(2,1)} %reshape.125), kind=kLoop, calls=%fused_computation.45 | loop fusion | bytes 9437184 | tf_op jit(solution)/shard_map/slice | solution.py:30
  338.6 0.6 copy.22
  339.2 0.7 slice.90
  339.9 1.2 slice.71
  341.1 2.2 slice.78
  343.2 1.0 slice.81
  344.2 3.6 reshape.109
  347.8 3.7 %reshape.110 = bf16[3,256,1024]{2,1,0:T(8,128)(2,1)} reshape(bf16[786432]{0:T(1024)(128)(2,1)} %get-tuple-element.37) | data formatting | bytes 3145728 | tf_op jit(solution)/shard_map/reshape | solution.py:30
  351.5 1.9 reshape.111
  353.5 0.6 reshape.113
  354.1 1.2 gather_fusion
  355.2 2.4 fusion
  (40 shorter events, 0.2 us)
Async XLA Ops:
  7.2 4.5 %copy-start.2 = (f32[1,3,4,256,256]{4,3,2,1,0:T(8,128)S(1)}, f32[1,3,4,256,256]{4,3,2,1,0:T(8,128)}, u32[]{:S(2)}) copy-start(f32[1,3,4,256,256]{4,3,2,1,0:T(8,128)} %param.12) | copy-start | bytes 9437188
  7.2 201.5 %all-reduce.4.cloned.1.call-start = ((), (), s32[]{:S(2)}) async-start(), calls=%async_computation.1 | async-start | bytes 23199744
  10.1 4.9 %copy-start.3 = (f32[1,3,256,1024]{3,2,1,0:T(8,128)S(1)}, f32[1,3,256,1024]{3,2,1,0:T(8,128)}, u32[]{:S(2)}) copy-start(f32[1,3,256,1024]{3,2,1,0:T(8,128)} %param.13) | copy-start | bytes 9437188
  11.7 5.7 %copy-start.4 = (f32[1,3,1024,256]{3,2,1,0:T(8,128)S(1)}, f32[1,3,1024,256]{3,2,1,0:T(8,128)}, u32[]{:S(2)}) copy-start(f32[1,3,1024,256]{3,2,1,0:T(8,128)} %param.14) | copy-start | bytes 9437188
  14.9 4.0 %copy-start.9 = (f32[1,3,9,256]{3,0,2,1:T(1,128)S(1)}, f32[1,3,9,256]{3,0,2,1:T(1,128)}, u32[]{:S(2)}) copy-start(f32[1,3,9,256]{3,0,2,1:T(1,128)} %param.15) | copy-start | bytes 82948
  19.1 3.9 %copy-start = (f32[96,8,8,128]{3,1,2,0:T(8,128)S(1)}, f32[96,8,8,128]{3,1,2,0:T(8,128)}, u32[]{:S(2)}) copy-start(f32[96,8,8,128]{3,1,2,0:T(8,128)} %copy.25) | copy-start | bytes 9437188
  23.0 5.1 %copy-start.10 = (f32[1,3,1024]{2,0,1:T(1,128)S(1)}, f32[1,3,1024]{2,0,1:T(1,128)}, u32[]{:S(2)}) copy-start(f32[1,3,1024]{2,0,1:T(1,128)} %param.16) | copy-start | bytes 36868
  39.4 169.3 %copy-start.6 = (f32[22656]{0:T(1024)S(1)}, f32[22656]{0:T(1024)}, u32[]{:S(2)}) copy-start(f32[22656]{0:T(1024)} %param.19) | copy-start | bytes 271876
  39.4 169.3 %copy-start.7 = (f32[22656]{0:T(1024)S(1)}, f32[22656]{0:T(1024)}, u32[]{:S(2)}) copy-start(f32[22656]{0:T(1024)} %param.18) | copy-start | bytes 271876
  39.4 169.3 %copy-start.8 = (f32[22656]{0:T(1024)S(1)}, f32[22656]{0:T(1024)}, u32[]{:S(2)}) copy-start(f32[22656]{0:T(1024)} %param.17) | copy-start | bytes 271876
  39.4 171.7 %copy-start.11 = (s32[256]{0:T(256)S(1)}, s32[256]{0:T(256)}, u32[]{:S(2)}) copy-start(s32[256]{0:T(256)} %param.20) | copy-start | bytes 3076
  39.5 243.7 %all-gather.3.cloned.1.call-start = ((), (), s32[]{:S(2)}) async-start(), calls=%async_computation | async-start | bytes 11690496 | tf_op jit(solution)/shard_map/all_gather | solution.py:55
  331.4 7.2 %slice-start.1 = ((bf16[2899968]{0:T(1024)(128)(2,1)}), bf16[6912]{0:T(1024)(128)(2,1)S(1)}, s32[]{:S(2)}) async-start(bf16[2899968]{0:T(1024)(128)(2,1)} %reshape.125), calls=%async_computation.3 | async-start | bytes 28672 | tf_op jit(solution)/shard_map/slice | solution.py:30
  331.4 8.5 %slice-start = ((bf16[2899968]{0:T(1024)(128)(2,1)}), bf16[524288]{0:T(1024)(128)(2,1)S(1)}, s32[]{:S(2)}) async-start(bf16[2899968]{0:T(1024)(128)(2,1)} %reshape.125), calls=%async_computation.2 | async-start | bytes 2097152 | tf_op jit(solution)/shard_map/slice | solution.py:30
  341.1 13.0 %copy-start.1 = (bf16[2048,256]{1,0:T(8,128)(2,1)S(1)}, bf16[2048,256]{1,0:T(8,128)(2,1)}, u32[]{:S(2)}) copy-start(bf16[2048,256]{1,0:T(8,128)(2,1)} %slice.71) | copy-start | bytes 3145732
  343.2 12.0 %copy-start.12 = (bf16[256,256]{1,0:T(8,128)(2,1)S(1)}, bf16[256,256]{1,0:T(8,128)(2,1)}, u32[]{:S(2)}) copy-start(bf16[256,256]{1,0:T(8,128)(2,1)} %param.21) | copy-start | bytes 393220
  344.2 11.0 %copy-start.5 = (bf16[256,1024]{1,0:T(8,128)(2,1)S(1)}, bf16[256,1024]{1,0:T(8,128)(2,1)}, u32[]{:S(2)}) copy-start(bf16[256,1024]{1,0:T(8,128)(2,1)} %slice.78) | copy-start | bytes 1572868
Sparse Core Ops, SparseCore 0:
  39.6 169.0 all-reduce.3
  212.3 70.9 all-gather.2
where the time goes:
time: 365 us; the launch traced here: 364 us
  waiting for transfers between devices  241 us (66%)
  local copies, waits for them, and re-layouts  67.7 us (19%)
  other arithmetic  38.9 us (11%)
  between operations  14.2 us (4%)
    unnamed x3, waiting for transfers between devices  169 us
    all_gather x1, waiting for transfers between devices, device_step(): lax.all_gather(w_new.astype(jnp.bfloat16), AXES, axis=0, tiled=True)  72 us
    all_gather x1, other arithmetic, device_step(): lax.all_gather(w_new.astype(jnp.bfloat16), AXES, axis=0, tiled=True)  36.4 us
    unnamed x38, local copies, waits for them, and re-layouts  33.9 us
    pad x1, local copies, waits for them, and re-layouts, device_step(): local_flat = jnp.pad(local_flat, (0, shard_len * devices - param_count))  10 us
    reshape x5, local copies, waits for them, and re-layouts, split_flat(): pieces.append(flat_vals[offset:offset + elem_count].reshape(tensor_shape))  9.89 us
  transfers between devices with their start and end apart: 2, of which 2 were waited for; matrix products, arithmetic and copies ran while one was open for 0% of the time, Pallas kernels for 0%

commit v1 on v0

v1 whole, which is shorter than its diff:
```python
import functools
import math
import jax
import jax.numpy as jnp
from jax import lax
from jax.experimental import pallas as pl
from jax.experimental.pallas import tpu as pltpu
from jax.sharding import PartitionSpec as P

LEARN_RATE = 0.002
BETA_ONE = 0.9
BETA_TWO = 0.95
ADAM_EPS = 1e-8
ADAM_STEP = 2
AXES = ("dz", "dy", "dx")
GRAD_RANKS = (3, 5, 4, 4, 4, 3)
MESH = pl.DeviceIdType.MESH

SHARD = 177
PART = 59
APART = 60
ROWS = 22656
REAL = 22606
BASE = (0, 4096, 10240, 16384, 22528, 22582)
GROUPS = (256, 384, 96, 384)
TILES = (2, 2, 8, 2)
ORDER = ((0, 1, 2), (1, 2, 0), (2, 0, 1))
F32 = jnp.float32
BF16 = jnp.bfloat16


def loop(count, body, unroll=1):
    def step(i, carry):
        body(i)
        return carry
    lax.fori_loop(0, count, step, 0, unroll=unroll)


def shard_of(k, q1, q2, q3, core):
    pos = [None] * 3
    for axis, q in zip(ORDER[k], (q1, q2, q3)):
        pos[axis] = q
    return pos[2] * 32 + pos[1] * 8 + pos[0] * 2 + core


def sync_kernel(e_hbm, a_hbm, i_hbm, o_hbm, vd_hbm, vf_hbm, m_ref, v_ref, w_ref,
                m_out, v_out, w_out, ag,
                e_raw, a_raw, i_raw, o_raw, vd_raw, vf_raw, flat, psl, work, drx,
                r1, r2, r3,
                raw_sem, dsend, drecv, ssend, srecv, asend, arecv, gsend, grecv):
    dz, dy, dx = lax.axis_index("dz"), lax.axis_index("dy"), lax.axis_index("dx")
    core = lax.rem(dx, 2)
    pos = (lax.div(dx, 2), dy, dz)
    partner = {"dz": dz, "dy": dy, "dx": dx + 1 - 2 * core}

    def neighbour(axis, shift):
        q = lax.rem(pos[axis] + 4 + shift, 4)
        if axis == 0:
            return {"dz": dz, "dy": dy, "dx": q * 2 + core}
        if axis == 1:
            return {"dz": dz, "dy": q, "dx": dx}
        return {"dz": q, "dy": dy, "dx": dx}

    def ring(axis, shift):
        return lax.rem(pos[axis] + 4 + shift, 4)

    barrier = pltpu.get_barrier_semaphore()
    for axis in range(3):
        for shift in (1, -1):
            pl.semaphore_signal(barrier, inc=1, device_id=neighbour(axis, shift), device_id_type=MESH)
    pl.semaphore_signal(barrier, inc=1, device_id=partner, device_id_type=MESH)

    raws = (e_raw, a_raw, i_raw, o_raw, vd_raw, vf_raw)
    loads = [pltpu.make_async_copy(src, dst, raw_sem.at[n]) for n, (src, dst) in enumerate(
        zip((e_hbm, a_hbm, i_hbm, o_hbm, vd_hbm, vf_hbm), raws))]
    for n in (0, 1, 2, 3, 4, 5):
        loads[n].start()

    flat[pl.ds(REAL, ROWS - REAL), :] = jnp.zeros((ROWS - REAL, 128), F32)
    for n in range(4):
        loads[n].wait()
        tiles, base, raw = TILES[n], BASE[n], raws[n]

        def relayout(g, tiles=tiles, base=base, raw=raw):
            for c in range(tiles):
                flat[pl.ds(base + g * (8 * tiles) + c, 8, stride=tiles), :] = raw[g, c]
        loop(GROUPS[n], relayout, unroll=16 // tiles)
    loads[4].wait()
    flat[pl.ds(BASE[4], 54), :] = vd_raw[...]
    loads[5].wait()
    flat[pl.ds(BASE[5], 24), :] = vf_raw[...]

    pl.semaphore_wait(barrier, 7)

    def flat_row(k, q1, j, c):
        return SHARD * shard_of(k, q1, lax.div(j, 4), lax.rem(j, 4), c) + PART * k

    def d2d(k, q1):
        return pltpu.make_async_remote_copy(
            src_ref=psl.at[k, q1], dst_ref=drx.at[k, q1],
            send_sem=dsend.at[k, q1], recv_sem=drecv.at[k, q1],
            device_id=partner, device_id_type=MESH)

    for shift in (2, 1, -1, 0):
        for k in range(3):
            q1 = ring(ORDER[k][0], shift)

            def pick(j, k=k, q1=q1):
                psl[k, q1, j] = flat[pl.ds(flat_row(k, q1, j, 1 - core), PART), :]
            loop(16, pick, unroll=2)
            d2d(k, q1).start()

    def add_core(k, shift):
        q1 = ring(ORDER[k][0], shift)
        d2d(k, q1).wait_recv()

        def body(j):
            work[k, q1, j] = flat[pl.ds(flat_row(k, q1, j, core), PART), :] + drx[k, q1, j]
        loop(16, body, unroll=2)

    def chunk(t, k, shift, half):
        p = [pos[a] for a in ORDER[k]]
        q = ring(ORDER[k][t], shift)
        if t == 0:
            return work.at[k, q, pl.ds(8 * half, 8)]
        if t == 1:
            return work.at[k, p[0], pl.ds(4 * q + 2 * half, 2)]
        return work.at[k, p[0], 4 * p[1] + q, pl.ds(32 * half, 32 - 5 * half)]

    def landing(t, k, part, half):
        if t == 0:
            return r1.at[k, part]
        if t == 1:
            return r2.at[k, part]
        return r3.at[k, part, pl.ds(0, 32 - 5 * half)]

    PARTS = ((2, 0, 1), (2, 1, -1), (1, 1, 1), (1, 0, 1), (-1, 0, -1), (-1, 1, -1))

    def rs(t, k, part):
        shift, half, way = PARTS[part]
        return pltpu.make_async_remote_copy(
            src_ref=chunk(t, k, shift, half), dst_ref=landing(t, k, part, half),
            send_sem=ssend.at[t, k, part], recv_sem=srecv.at[t, k, part],
            device_id=neighbour(ORDER[k][t], way), device_id_type=MESH)

    def accumulate(t, k, shift, half, part):
        rs(t, k, part).wait_recv()
        dst = chunk(t, k, shift, half)
        src = landing(t, k, part, half)
        if t == 0:
            def body(j):
                dst[j] = dst[j] + src[j]
            loop(8, body, unroll=2)
        else:
            dst[...] = dst[...] + src[...]

    colours = range(3)
    for t in range(3):
        if t == 0:
            for k in colours:
                add_core(k, 2)
                rs(t, k, 0).start()
                rs(t, k, 1).start()
            for k in colours:
                add_core(k, 1)
                rs(t, k, 2).start()
                add_core(k, -1)
                rs(t, k, 4).start()
        else:
            for k in colours:
                rs(t, k, 0).start()
                rs(t, k, 1).start()
                rs(t, k, 2).start()
                rs(t, k, 4).start()
        for k in colours:
            accumulate(t, k, 1, 0, 0)
            rs(t, k, 3).start()
            accumulate(t, k, -1, 1, 1)
            rs(t, k, 5).start()
        if t == 0:
            for k in colours:
                add_core(k, 0)
        for k in colours:
            accumulate(t, k, 0, 1, 2)
            accumulate(t, k, 0, 0, 4)
        for k in colours:
            accumulate(t, k, 0, 0, 3)
            accumulate(t, k, 0, 1, 5)

    for k in colours:
        p = [pos[a] for a in ORDER[k]]
        rows = pl.ds(PART * k, PART)
        grad = work[k, p[0], 4 * p[1] + p[2]] * (1.0 / 128.0)
        m_new = BETA_ONE * m_ref[rows, :] + (1.0 - BETA_ONE) * grad
        v_new = BETA_TWO * v_ref[rows, :] + (1.0 - BETA_TWO) * grad * grad
        m_hat = m_new / (1.0 - BETA_ONE ** ADAM_STEP)
        v_hat = v_new / (1.0 - BETA_TWO ** ADAM_STEP)
        m_out[rows, :] = m_new
        v_out[rows, :] = v_new
        w_out[rows, :] = w_ref[rows, :] - LEARN_RATE * m_hat / (jnp.sqrt(v_hat) + ADAM_EPS)
    for k in colours:
        p = [pos[a] for a in ORDER[k]]
        own = 16 * p[0] + 4 * p[1] + p[2]
        if k < 2:
            ag[k, core, own] = w_out[pl.ds(APART * k, APART), :].astype(BF16)
        else:
            vals = jnp.concatenate([w_out[pl.ds(120, 57), :], jnp.zeros((3, 128), F32)], axis=0)
            ag[k, core, own] = vals.astype(BF16)

    def block(t, k, shift, half=None):
        p = [pos[a] for a in ORDER[k]]
        q = ring(ORDER[k][t], shift)
        size = (16, 4, 1)[t]
        start = (16 * q, 16 * p[0] + 4 * q, 16 * p[0] + 4 * p[1] + q)[t]
        if t == 2:
            at = ag.at[k, core, start]
            if half is None:
                return at
            return at.at[pl.ds(32 * half, 32 - 4 * half)]
        if half is not None:
            size = size // 2
            start = start + size * half
        return ag.at[k, core, pl.ds(start, size)]

    GPARTS = ((0, None, 1), (0, None, -1), (-1, 0, 1), (1, 1, -1))

    def gather(t, k, part, came=0):
        shift, half, way = GPARTS[part]
        ref = block(t, k, shift - came, half)
        return pltpu.make_async_remote_copy(
            src_ref=ref, dst_ref=ref,
            send_sem=asend.at[t, k, part], recv_sem=arecv.at[t, k, part],
            device_id=neighbour(ORDER[k][t], way), device_id_type=MESH)

    def arrived(t, k, part):
        gather(t, k, part, came=GPARTS[part][2]).wait_recv()

    def share(k, shift):
        q = ring(ORDER[k][0], shift)
        ref = ag.at[k, core, pl.ds(16 * q, 16)]
        return pltpu.make_async_remote_copy(
            src_ref=ref, dst_ref=ref,
            send_sem=gsend.at[k, q], recv_sem=grecv.at[k, q],
            device_id=partner, device_id_type=MESH)

    def shared(k, shift):
        q = ring(ORDER[k][0], shift)
        ref = ag.at[k, 1 - core, pl.ds(16 * q, 16)]
        pltpu.make_async_remote_copy(
            src_ref=ref, dst_ref=ref,
            send_sem=gsend.at[k, q], recv_sem=grecv.at[k, q],
            device_id=partner, device_id_type=MESH).wait_recv()

    for t in (2, 1, 0):
        for k in colours:
            gather(t, k, 0).start()
            gather(t, k, 1).start()
            if t == 0:
                share(k, 0).start()
        for k in colours:
            arrived(t, k, 0)
            gather(t, k, 2).start()
            arrived(t, k, 1)
            gather(t, k, 3).start()
            if t == 0:
                share(k, -1).start()
                share(k, 1).start()
        for k in colours:
            arrived(t, k, 2)
            arrived(t, k, 3)
            if t == 0:
                share(k, 2).start()
    for shift in (0, -1, 1, 2):
        for k in colours:
            shared(k, shift)

    for k in colours:
        for shift in (0, -1, 1, 2):
            d2d(k, ring(ORDER[k][0], shift)).wait_send()
            share(k, shift).wait_send()
        for t in range(3):
            for part in range(6):
                rs(t, k, part).wait_send()
            for part in range(4):
                gather(t, k, part).wait_send()


def apply_kernel(ids, ag, act, emb_out, attn_out, in_out, ff_out, vd_out, vf_out, y_out,
                 flat, emb_v, attn_v, in_v, out_v, vd_v, vf_v, rows_v, sems):
    for k in range(3):
        for c in range(2):
            def unpack(i, k=k, c=c):
                q1, q2, q3 = lax.div(i, 16), lax.rem(lax.div(i, 4), 4), lax.rem(i, 4)
                row = SHARD * shard_of(k, q1, q2, q3, c) + APART * k
                size = APART if k < 2 else 57
                flat[pl.ds(row, size), :] = ag[k, c, i].astype(F32)[:size]
            loop(64, unpack, unroll=2)

    stage = (emb_v, attn_v, in_v, out_v)
    outs = (emb_out, attn_out, in_out, ff_out)
    copies = []
    for n in range(4):
        tiles, base, dst = TILES[n], BASE[n], stage[n]

        def pack(g, tiles=tiles, base=base, dst=dst):
            rows = pl.ds(pl.multiple_of(16 * g, 16), 16)
            for c in range(tiles):
                vals = flat[pl.ds(base + g * (16 * tiles) + c, 16, stride=tiles), :]
                dst[rows, 128 * c:128 * c + 128] = vals.astype(BF16)
        loop(GROUPS[n] // 2, pack, unroll=8 // tiles)
        copy = pltpu.make_async_copy(dst, outs[n], sems.at[n])
        copy.start()
        copies.append(copy)
    vd_v[...] = flat[pl.ds(BASE[4], 54), :].astype(BF16)
    vf_v[...] = flat[pl.ds(BASE[5], 24), :].astype(BF16)
    for n, (src, dst) in enumerate(((vd_v, vd_out), (vf_v, vf_out))):
        copy = pltpu.make_async_copy(src, dst, sems.at[4 + n])
        copy.start()
        copies.append(copy)

    def look(i):
        rows_v[pl.ds(2 * i, 2), :] = flat[pl.ds(2 * ids[i], 2), :]
    loop(256, look, unroll=8)
    def bias(row, count):
        flat_vals = flat[pl.ds(row, count), :].astype(BF16).astype(F32)
        return jnp.concatenate([flat_vals[i:i + 1] for i in range(count)], axis=1)
    emb = jnp.concatenate([rows_v[pl.ds(0, 256, stride=2), :], rows_v[pl.ds(1, 256, stride=2), :]], axis=1)
    hidden = (emb * 16.0 + act[...].astype(F32)).astype(BF16)
    pre = jnp.dot(hidden, in_v[0:256, :], preferred_element_type=F32) + bias(BASE[5], 8)
    inner = jax.nn.gelu(pre, approximate=True).astype(BF16)
    y = jnp.dot(inner, out_v[0:1024, :], preferred_element_type=F32) + bias(BASE[4] + 16, 2)
    y_out[...] = y.astype(BF16)
    for copy in copies:
        copy.wait()


def tiled(grad, width):
    flat = grad.reshape(-1, 8, width // 128, 128)
    return flat.transpose(0, 2, 1, 3)


def solution(mesh):
    def device_step(g_emb, g_attn, g_in, g_out, g_vecd, g_vecf, opt_m, opt_v, master, tok_ids, act_in):
        shapes = [g.shape[1:] for g in (g_emb, g_attn, g_in, g_out, g_vecd, g_vecf)]
        grads = (tiled(g_emb, 256), tiled(g_attn, 256), tiled(g_in, 1024), tiled(g_out, 256),
                 g_vecd.reshape(54, 128), g_vecf.reshape(24, 128))
        state = [s.reshape(SHARD, 128) for s in (opt_m, opt_v, master)]
        anywhere = pl.BlockSpec(memory_space=pltpu.HBM)
        vmem = pl.BlockSpec(memory_space=pltpu.VMEM)
        slots = pltpu.VMEM((3, 4, 16, PART, 128), F32)
        dma = pltpu.SemaphoreType.DMA
        shard = jax.ShapeDtypeStruct((SHARD, 128), F32)
        m_new, v_new, w_new, gathered = pl.pallas_call(
            sync_kernel,
            name="sync",
            out_shape=(shard, shard, shard, jax.ShapeDtypeStruct((3, 2, 64, APART, 128), BF16)),
            in_specs=[anywhere] * 6 + [vmem] * 3,
            out_specs=[vmem] * 4,
            scratch_shapes=[pltpu.VMEM(g.shape, F32) for g in grads] + [
                pltpu.VMEM((ROWS, 128), F32), slots, slots, slots,
                pltpu.VMEM((3, 6, 8, PART, 128), F32),
                pltpu.VMEM((3, 6, 2, PART, 128), F32),
                pltpu.VMEM((3, 6, 32, 128), F32),
                dma((6,)), dma((3, 4)), dma((3, 4)), dma((3, 3, 6)), dma((3, 3, 6)),
                dma((3, 3, 4)), dma((3, 3, 4)), dma((3, 4)), dma((3, 4))],
            compiler_params=pltpu.CompilerParams(
                collective_id=0, has_side_effects=True, vmem_limit_bytes=67043328),
        )(*grads, *state)

        flat_shapes = [(2048, 256), (3072, 256), (768, 1024), (3072, 256), (54, 128), (24, 128)]
        outs = pl.pallas_call(
            apply_kernel,
            name="apply",
            out_shape=[jax.ShapeDtypeStruct(s, BF16) for s in flat_shapes + [(256, 256)]],
            in_specs=[pl.BlockSpec(memory_space=pltpu.SMEM), vmem, vmem],
            out_specs=[anywhere] * 6 + [vmem],
            scratch_shapes=[pltpu.VMEM((ROWS, 128), F32)] + [pltpu.VMEM(s, BF16) for s in flat_shapes] + [
                pltpu.VMEM((512, 128), F32), dma((6,))],
            compiler_params=pltpu.CompilerParams(vmem_limit_bytes=67043328),
        )(tok_ids, gathered, act_in)
        halves = [o.reshape(s) for o, s in zip(outs[:6], shapes)]
        return (m_new.reshape(-1), v_new.reshape(-1), w_new.reshape(-1), *halves, outs[6])

    grad_specs = tuple(P(AXES, *([None] * (grad_rank - 1))) for grad_rank in GRAD_RANKS)
    in_specs = grad_specs + (P(AXES), P(AXES), P(AXES), P(AXES), P(AXES, None))
    out_specs = (P(AXES), P(AXES), P(AXES), P(), P(), P(), P(), P(), P(), P(AXES, None))
    return jax.shard_map(device_step, mesh=mesh, in_specs=in_specs, out_specs=out_specs, check_vma=False)
```

time: 365 us -> 101 us (0.28)
  waiting for transfers between devices: 241 us -> 0 us
  Pallas kernels: 0 us -> 90.9 us
  local copies, waits for them, and re-layouts: 67.7 us -> 7.87 us
  other arithmetic: 38.9 us -> 0.81 us
  between operations: 14.2 us -> 0.67 us
    unnamed x3 -> x0, waiting for transfers between devices: 169 us -> none
    pallas_call x0 -> x2, Pallas kernels: none -> 90.9 us  [the longest x1 80.5 us: device_step(): pl.pallas_call(sync_kernel, name='sync', out_shape=(shard, shard, shard,...]
    all_gather x1 -> x0, waiting for transfers between devices: 72 us -> none  [device_step(): lax.all_gather(w_new.astype(jnp.bfloat16), AXES, axis=0, tiled=True)]
    all_gather x1 -> x0, other arithmetic: 36.4 us -> none  [device_step(): lax.all_gather(w_new.astype(jnp.bfloat16), AXES, axis=0, tiled=True)]
    unnamed x38 -> x4, local copies, waits for them, and re-layouts: 33.9 us -> 5.22 us
    slice x10 -> x0, local copies, waits for them, and re-layouts: 11.4 us -> none  [the longest x7 6.18 us: split_flat(): pieces.append(flat_vals[offset:offset + elem_count].reshape(tensor_shape))]
    pad x1 -> x0, local copies, waits for them, and re-layouts: 10 us -> none  [device_step(): local_flat = jnp.pad(local_flat, (0, shard_len * devices - param_count))]
    reshape x6 -> x3, local copies, waits for them, and re-layouts: 9.89 us -> 2.65 us  [the longest x2 2.03 us: device_step(): halves = [o.reshape(s) for o, s in zip(outs[:6], shapes)]]
  transfers between devices with their start and end apart: 2 -> 0, of which waited for: 2 -> 0; matrix products, arithmetic and copies ran while one was open for 0% -> 0% of each run, Pallas kernels for 0% -> 0%
where the time goes in v1:
time: 101 us; the launch traced here: 100 us
  Pallas kernels  90.9 us (90%)
  local copies, waits for them, and re-layouts  7.87 us (8%)
    pallas_call x1, Pallas kernels, device_step(): pl.pallas_call(sync_kernel, name='sync', out_shape=(shard, shard, shard,...  80.5 us
    pallas_call x1, Pallas kernels, device_step(): pl.pallas_call(apply_kernel, name='apply', out_shape=[jax.ShapeDtypeStruc...  10.5 us
    unnamed x4, local copies, waits for them, and re-layouts  5.22 us
    reshape x2, local copies, waits for them, and re-layouts, device_step(): halves = [o.reshape(s) for o, s in zip(outs[:6], shapes)]  2.03 us

profile of v1, /device:TPU:1, one launch (start us, length us, event | category | flops | bytes accessed | tf_op | source)
XLA Modules:
  0.0 100.3 jit_solution(6196015127422254589)
XLA Ops:
  0.6 0.8 reduce
  1.5 0.6 reshape.75.vd_hbm
  2.1 80.5 %sync.1 = (f32[177,128]{1,0:T(8,128)}, f32[177,128]{1,0:T(8,128)}, f32[177,128]{1,0:T(8,128)}, bf16[3,2,64,60,128]{4,3,2,1,0:T(8,128)(2,1)}) custom-call(f32[256,2,8,128]{3,2,1,0:T(8,128)} %bitcast.25, f32[384,2,8,128]{3,2,1,0:T(8,128)} %bitcast.22, f32[96,8,8,128]{3,2,1,0:T(8,128)} %bitcast.23, f32[384,2,8,128]{3,2,1,0:T(8,128)} %bitcast.24, ...), custom_call_target="tpu_custom_call" | custom-call | tf_op jit(solution)/shard_map/sync/pallas_call | solution.py:353
  82.5 10.5 %apply.1 = (bf16[2048,256]{1,0:T(8,128)(2,1)}, bf16[3072,256]{1,0:T(8,128)(2,1)}, bf16[768,1024]{1,0:T(8,128)(2,1)}, bf16[3072,256]{1,0:T(8,128)(2,1)}, bf16[54,...) custom-call(s32[256]{0:T(256)} %ids.1, bf16[3,2,64,60,128]{4,3,2,1,0:T(8,128)(2,1)} %get-tuple-element.24.ag, ...), custom_call_target="tpu_custom_call" | custom-call | tf_op jit(solution)/shard_map/apply/pallas_call | solution.py:371
  93.0 1.3 %reshape.87 = bf16[3,1024]{1,0:T(4,128)(2,1)} reshape(bf16[24,128]{1,0:T(8,128)(2,1)} %get-tuple-element.30) | data formatting | bytes 12288 | tf_op jit(solution)/shard_map/reshape | solution.py:381
  94.3 0.7 reshape.86
  95.0 0.6 copy.22
  95.7 1.5 %copy.26 = f32[22656]{0:T(1024)} copy(f32[22656]{0:T(1024)} %bitcast.31) | data formatting | bytes 181248
  97.2 1.5 %copy.27 = f32[22656]{0:T(1024)} copy(f32[22656]{0:T(1024)} %bitcast.30) | data formatting | bytes 181248
  98.7 1.5 %copy.28 = f32[22656]{0:T(1024)} copy(f32[22656]{0:T(1024)} %bitcast.29) | data formatting | bytes 181248

commit v2 on v1

--- a/solution.py
+++ b/solution.py
@@ -44,8 +44,8 @@
 
 
 def sync_kernel(e_hbm, a_hbm, i_hbm, o_hbm, vd_hbm, vf_hbm, m_ref, v_ref, w_ref,
-                m_out, v_out, w_out, ag,
-                e_raw, a_raw, i_raw, o_raw, vd_raw, vf_raw, flat, psl, work, drx,
+                m_out, v_out, w_out, flat,
+                e_raw, a_raw, i_raw, o_raw, vd_raw, vf_raw, ag, psl, work, drx,
                 r1, r2, r3,
                 raw_sem, dsend, drecv, ssend, srecv, asend, arecv, gsend, grecv):
     dz, dy, dx = lax.axis_index("dz"), lax.axis_index("dy"), lax.axis_index("dx")
@@ -86,7 +86,9 @@
                 flat[pl.ds(base + g * (8 * tiles) + c, 8, stride=tiles), :] = raw[g, c]
         loop(GROUPS[n], relayout, unroll=16 // tiles)
     loads[4].wait()
-    flat[pl.ds(BASE[4], 54), :] = vd_raw[...]
+    for i in range(27):
+        for h in range(2):
+            flat[pl.ds(BASE[4] + 2 * i + h, 1), :] = vd_raw[i, :, 128 * h:128 * h + 128]
     loads[5].wait()
     flat[pl.ds(BASE[5], 24), :] = vf_raw[...]
 
@@ -251,12 +253,24 @@
             send_sem=gsend.at[k, q], recv_sem=grecv.at[k, q],
             device_id=partner, device_id_type=MESH).wait_recv()
 
+    def unpack(k, c, shift):
+        q1 = ring(ORDER[k][0], shift)
+        size = APART if k < 2 else 57
+
+        def body(j):
+            row = SHARD * shard_of(k, q1, lax.div(j, 4), lax.rem(j, 4), c) + APART * k
+            flat[pl.ds(row, size), :] = ag[k, c, 16 * q1 + j].astype(F32)[:size]
+        loop(16, body, unroll=2)
+
     for t in (2, 1, 0):
         for k in colours:
             gather(t, k, 0).start()
             gather(t, k, 1).start()
             if t == 0:
                 share(k, 0).start()
+        if t == 0:
+            for k in colours:
+                unpack(k, core, 0)
         for k in colours:
             arrived(t, k, 0)
             gather(t, k, 2).start()
@@ -270,9 +284,13 @@
             arrived(t, k, 3)
             if t == 0:
                 share(k, 2).start()
+    for shift in (-1, 1, 2):
+        for k in colours:
+            unpack(k, core, shift)
     for shift in (0, -1, 1, 2):
         for k in colours:
             shared(k, shift)
+            unpack(k, 1 - core, shift)
 
     for k in colours:
         for shift in (0, -1, 1, 2):
@@ -285,20 +303,20 @@
                 gather(t, k, part).wait_send()
 
 
-def apply_kernel(ids, ag, act, emb_out, attn_out, in_out, ff_out, vd_out, vf_out, y_out,
-                 flat, emb_v, attn_v, in_v, out_v, vd_v, vf_v, rows_v, sems):
-    for k in range(3):
-        for c in range(2):
-            def unpack(i, k=k, c=c):
-                q1, q2, q3 = lax.div(i, 16), lax.rem(lax.div(i, 4), 4), lax.rem(i, 4)
-                row = SHARD * shard_of(k, q1, q2, q3, c) + APART * k
-                size = APART if k < 2 else 57
-                flat[pl.ds(row, size), :] = ag[k, c, i].astype(F32)[:size]
-            loop(64, unpack, unroll=2)
-
+def apply_kernel(ids, flat, act, m_in, v_in, w_in,
+                 emb_out, attn_out, in_out, ff_out, vd_out, vf_out, y_out, m_out, v_out, w_out,
+                 emb_v, attn_v, in_v, out_v, vd_v, vf_v, rows_v, sems):
+    copies = []
+
+    def send(src, dst):
+        copy = pltpu.make_async_copy(src, dst, sems.at[len(copies)])
+        copy.start()
+        copies.append(copy)
+
+    for src, dst in ((m_in, m_out), (v_in, v_out), (w_in, w_out)):
+        send(src, dst)
     stage = (emb_v, attn_v, in_v, out_v)
     outs = (emb_out, attn_out, in_out, ff_out)
-    copies = []
     for n in range(4):
         tiles, base, dst = TILES[n], BASE[n], stage[n]
 
@@ -308,19 +326,20 @@
                 vals = flat[pl.ds(base + g * (16 * tiles) + c, 16, stride=tiles), :]
                 dst[rows, 128 * c:128 * c + 128] = vals.astype(BF16)
         loop(GROUPS[n] // 2, pack, unroll=8 // tiles)
-        copy = pltpu.make_async_copy(dst, outs[n], sems.at[n])
-        copy.start()
-        copies.append(copy)
-    vd_v[...] = flat[pl.ds(BASE[4], 54), :].astype(BF16)
-    vf_v[...] = flat[pl.ds(BASE[5], 24), :].astype(BF16)
-    for n, (src, dst) in enumerate(((vd_v, vd_out), (vf_v, vf_out))):
-        copy = pltpu.make_async_copy(src, dst, sems.at[4 + n])
-        copy.start()
-        copies.append(copy)
+        send(dst, outs[n])
+    for r in range(9):
+        for h in range(2):
+            vals = flat[pl.ds(BASE[4] + 2 * r + h, 3, stride=18), :]
+            vd_v[r, :, 128 * h:128 * h + 128] = vals.astype(BF16)
+    for c in range(8):
+        vf_v[:, 128 * c:128 * c + 128] = flat[pl.ds(BASE[5] + c, 3, stride=8), :].astype(BF16)
+    send(vd_v, vd_out)
+    send(vf_v, vf_out)
 
     def look(i):
         rows_v[pl.ds(2 * i, 2), :] = flat[pl.ds(2 * ids[i], 2), :]
     loop(256, look, unroll=8)
+
     def bias(row, count):
         flat_vals = flat[pl.ds(row, count), :].astype(BF16).astype(F32)
         return jnp.concatenate([flat_vals[i:i + 1] for i in range(count)], axis=1)
@@ -343,43 +362,45 @@
     def device_step(g_emb, g_attn, g_in, g_out, g_vecd, g_vecf, opt_m, opt_v, master, tok_ids, act_in):
         shapes = [g.shape[1:] for g in (g_emb, g_attn, g_in, g_out, g_vecd, g_vecf)]
         grads = (tiled(g_emb, 256), tiled(g_attn, 256), tiled(g_in, 1024), tiled(g_out, 256),
-                 g_vecd.reshape(54, 128), g_vecf.reshape(24, 128))
+                 g_vecd.transpose(1, 2, 0, 3).reshape(27, 1, 256), g_vecf.reshape(24, 128))
         state = [s.reshape(SHARD, 128) for s in (opt_m, opt_v, master)]
         anywhere = pl.BlockSpec(memory_space=pltpu.HBM)
         vmem = pl.BlockSpec(memory_space=pltpu.VMEM)
         slots = pltpu.VMEM((3, 4, 16, PART, 128), F32)
         dma = pltpu.SemaphoreType.DMA
-        shard = jax.ShapeDtypeStruct((SHARD, 128), F32)
-        m_new, v_new, w_new, gathered = pl.pallas_call(
+        shard = pltpu.VMEM((SHARD, 128), F32)
+        m_new, v_new, w_new, flat = pl.pallas_call(
             sync_kernel,
             name="sync",
-            out_shape=(shard, shard, shard, jax.ShapeDtypeStruct((3, 2, 64, APART, 128), BF16)),
+            out_shape=(shard, shard, shard, pltpu.VMEM((ROWS, 128), F32)),
             in_specs=[anywhere] * 6 + [vmem] * 3,
             out_specs=[vmem] * 4,
             scratch_shapes=[pltpu.VMEM(g.shape, F32) for g in grads] + [
-                pltpu.VMEM((ROWS, 128), F32), slots, slots, slots,
+                pltpu.VMEM((3, 2, 64, APART, 128), BF16), slots, slots, slots,
                 pltpu.VMEM((3, 6, 8, PART, 128), F32),
                 pltpu.VMEM((3, 6, 2, PART, 128), F32),
                 pltpu.VMEM((3, 6, 32, 128), F32),
                 dma((6,)), dma((3, 4)), dma((3, 4)), dma((3, 3, 6)), dma((3, 3, 6)),
                 dma((3, 3, 4)), dma((3, 3, 4)), dma((3, 4)), dma((3, 4))],
             compiler_params=pltpu.CompilerParams(
-                collective_id=0, has_side_effects=True, vmem_limit_bytes=67043328),
+                collective_id=0, has_side_effects=True, vmem_limit_bytes=50 * 1048576),
         )(*grads, *state)
 
-        flat_shapes = [(2048, 256), (3072, 256), (768, 1024), (3072, 256), (54, 128), (24, 128)]
+        staged = [(2048, 256), (3072, 256), (768, 1024), (3072, 256), (9, 3, 256), (3, 1024)]
+        state_out = jax.ShapeDtypeStruct((SHARD, 128), F32)
         outs = pl.pallas_call(
             apply_kernel,
             name="apply",
-            out_shape=[jax.ShapeDtypeStruct(s, BF16) for s in flat_shapes + [(256, 256)]],
-            in_specs=[pl.BlockSpec(memory_space=pltpu.SMEM), vmem, vmem],
-            out_specs=[anywhere] * 6 + [vmem],
-            scratch_shapes=[pltpu.VMEM((ROWS, 128), F32)] + [pltpu.VMEM(s, BF16) for s in flat_shapes] + [
-                pltpu.VMEM((512, 128), F32), dma((6,))],
-            compiler_params=pltpu.CompilerParams(vmem_limit_bytes=67043328),
-        )(tok_ids, gathered, act_in)
-        halves = [o.reshape(s) for o, s in zip(outs[:6], shapes)]
-        return (m_new.reshape(-1), v_new.reshape(-1), w_new.reshape(-1), *halves, outs[6])
+            out_shape=[jax.ShapeDtypeStruct(s, BF16) for s in staged + [(256, 256)]] + [state_out] * 3,
+            in_specs=[pl.BlockSpec(memory_space=pltpu.SMEM)] + [vmem] * 5,
+            out_specs=[anywhere] * 6 + [vmem] + [anywhere] * 3,
+            scratch_shapes=[pltpu.VMEM(s, BF16) for s in staged] + [
+                pltpu.VMEM((512, 128), F32), dma((9,))],
+            compiler_params=pltpu.CompilerParams(vmem_limit_bytes=24 * 1048576),
+        )(tok_ids, flat, act_in, m_new, v_new, w_new)
+        halves = [o.reshape(s) for o, s in zip(outs[:4], shapes)]
+        halves += [outs[4].transpose(1, 0, 2), outs[5]]
+        return (*[o.reshape(-1) for o in outs[7:]], *halves, outs[6])
 
     grad_specs = tuple(P(AXES, *([None] * (grad_rank - 1))) for grad_rank in GRAD_RANKS)
     in_specs = grad_specs + (P(AXES), P(AXES), P(AXES), P(AXES), P(AXES, None))

time: 101 us -> 83.4 us (0.83)
  Pallas kernels: 90.9 us -> 82.5 us
  local copies, waits for them, and re-layouts: 7.87 us -> 0.01 us
    pallas_call x1, Pallas kernels: 10.5 us -> 4.59 us  [device_step(): pl.pallas_call(apply_kernel, name='apply', out_shape=[jax.ShapeDtypeStruc...]
    unnamed x4, local copies, waits for them, and re-layouts: 5.22 us -> 0.01 us
    reshape x3 -> x0, local copies, waits for them, and re-layouts: 2.65 us -> none  [the longest x2 2.03 us: device_step(): halves = [o.reshape(s) for o, s in zip(outs[:6], shapes)]]
    pallas_call x1, Pallas kernels: 80.5 us -> 77.9 us  [device_step(): pl.pallas_call(sync_kernel, name='sync', out_shape=(shard, shard, shard,...]
where the time goes in v2:
time: 83.4 us; the launch traced here: 83.2 us
  Pallas kernels  82.5 us (99%)
    pallas_call x1, Pallas kernels, device_step(): pl.pallas_call(sync_kernel, name='sync', out_shape=(shard, shard, shard,...  77.9 us
    pallas_call x1, Pallas kernels, device_step(): pl.pallas_call(apply_kernel, name='apply', out_shape=[jax.ShapeDtypeStruc...  4.59 us

profile of v2, /device:TPU:1, one launch (start us, length us, event | category | flops | bytes accessed | tf_op | source)
XLA Modules:
  0.0 83.2 jit_solution(5551266803466886850)
XLA Ops:
  0.6 0.0 copy-start
  0.7 0.0 copy-start.1
  0.7 77.9 %sync.1 = (f32[177,128]{1,0:T(8,128)S(1)}, f32[177,128]{1,0:T(8,128)S(1)}, f32[177,128]{1,0:T(8,128)S(1)}, f32[22656,128]{1,0:T(8,128)S(1)}) custom-call(f32[256,2,8,128]{3,2,1,0:T(8,128)} %bitcast.27, f32[384,2,8,128]{3,2,1,0:T(8,128)} %bitcast.24, f32[96,8,8,128]{3,2,1,0:T(8,128)} %bitcast.25, f32[384,2,8,128]{3,2,1,0:T(8,128)} %bitcast.26, ...), custom_call_target="tpu_custom_call" | custom-call | tf_op jit(solution)/shard_map/sync/pallas_call | solution.py:372
  78.5 0.0 copy-done
  78.6 0.0 copy-done.1
  78.6 4.6 %apply.1 = (bf16[2048,256]{1,0:T(8,128)(2,1)}, bf16[3072,256]{1,0:T(8,128)(2,1)}, bf16[768,1024]{1,0:T(8,128)(2,1)}, bf16[3072,256]{1,0:T(8,128)(2,1)}, bf16[9,3...) custom-call(s32[256]{0:T(256)S(1)} %copy-done.1, ...), custom_call_target="tpu_custom_call" | custom-call | tf_op jit(solution)/shard_map/apply/pallas_call | solution.py:391
Async XLA Ops:
  0.6 77.9 %copy-start = (bf16[256,256]{1,0:T(8,128)(2,1)S(1)}, bf16[256,256]{1,0:T(8,128)(2,1)}, u32[]{:S(2)}) copy-start(bf16[256,256]{1,0:T(8,128)(2,1)} %act.1) | copy-start | bytes 393220
  0.7 77.9 %copy-start.1 = (s32[256]{0:T(256)S(1)}, s32[256]{0:T(256)}, u32[]{:S(2)}) copy-start(s32[256]{0:T(256)} %ids.1) | copy-start | bytes 3076

commit v3 on v2

v3 whole, which is shorter than its diff:
```python
import functools
import math
import jax
import jax.numpy as jnp
from jax import lax
from jax.experimental import pallas as pl
from jax.experimental.pallas import tpu as pltpu
from jax.sharding import PartitionSpec as P

LEARN_RATE = 0.002
BETA_ONE = 0.9
BETA_TWO = 0.95
ADAM_EPS = 1e-8
ADAM_STEP = 2
AXES = ("dz", "dy", "dx")
GRAD_RANKS = (3, 5, 4, 4, 4, 3)
MESH = pl.DeviceIdType.MESH

SHARD = 177
PART = 59
APART = 60
ROWS = 22656
REAL = 22606
BASE = (0, 4096, 10240, 16384, 22528, 22582)
GROUPS = (256, 384, 96, 384)
TILES = (2, 2, 8, 2)
ORDER = ((0, 1, 2), (1, 2, 0), (2, 0, 1))
F32 = jnp.float32
BF16 = jnp.bfloat16


def loop(count, body, unroll=1):
    def step(i, carry):
        body(i)
        return carry
    lax.fori_loop(0, count, step, 0, unroll=unroll)


def shard_of(k, q1, q2, q3, core):
    pos = [None] * 3
    for axis, q in zip(ORDER[k], (q1, q2, q3)):
        pos[axis] = q
    return pos[2] * 32 + pos[1] * 8 + pos[0] * 2 + core


def sync_kernel(e_hbm, a_hbm, i_hbm, o_hbm, vd_hbm, vf_hbm, m_ref, v_ref, w_ref,
                m_out, v_out, w_out, flat,
                e_raw, a_raw, i_raw, o_raw, vd_raw, vf_raw, ag, psl, work, drx,
                r1, r2, r3,
                raw_sem, dsend, drecv, s1send, s1recv, s2send, s2recv, s3send, s3recv,
                g2send, g2recv, g1send, g1recv, g0send, g0recv, shsend, shrecv):
    dz, dy, dx = lax.axis_index("dz"), lax.axis_index("dy"), lax.axis_index("dx")
    core = lax.rem(dx, 2)
    pos = (lax.div(dx, 2), dy, dz)
    partner = {"dz": dz, "dy": dy, "dx": dx + 1 - 2 * core}
    colours = range(3)
    FAR = (2, 1, -1, 0)

    def neighbour(axis, shift):
        q = lax.rem(pos[axis] + 4 + shift, 4)
        if axis == 0:
            return {"dz": dz, "dy": dy, "dx": q * 2 + core}
        if axis == 1:
            return {"dz": dz, "dy": q, "dx": dx}
        return {"dz": q, "dy": dy, "dx": dx}

    def ring(axis, shift):
        return lax.rem(pos[axis] + 4 + shift, 4)

    def remote(src, dst, send_sem, recv_sem, device):
        return pltpu.make_async_remote_copy(
            src_ref=src, dst_ref=dst, send_sem=send_sem, recv_sem=recv_sem,
            device_id=device, device_id_type=MESH)

    barrier = pltpu.get_barrier_semaphore()
    for axis in range(3):
        for shift in (1, -1, 2):
            pl.semaphore_signal(barrier, inc=1, device_id=neighbour(axis, shift), device_id_type=MESH)
    pl.semaphore_signal(barrier, inc=1, device_id=partner, device_id_type=MESH)

    raws = (e_raw, a_raw, i_raw, o_raw, vd_raw, vf_raw)
    loads = [pltpu.make_async_copy(src, dst, raw_sem.at[n]) for n, (src, dst) in enumerate(
        zip((e_hbm, a_hbm, i_hbm, o_hbm, vd_hbm, vf_hbm), raws))]
    for n in (0, 1, 2, 3, 4, 5):
        loads[n].start()

    flat[pl.ds(REAL, ROWS - REAL), :] = jnp.zeros((ROWS - REAL, 128), F32)
    for n in range(4):
        with jax.named_scope(f"load{n}"):
            loads[n].wait()
        tiles, base, raw = TILES[n], BASE[n], raws[n]

        def relayout(g, tiles=tiles, base=base, raw=raw):
            for c in range(tiles):
                flat[pl.ds(base + g * (8 * tiles) + c, 8, stride=tiles), :] = raw[g, c]
        loop(GROUPS[n], relayout, unroll=16 // tiles)
    loads[4].wait()
    for i in range(27):
        for h in range(2):
            flat[pl.ds(BASE[4] + 2 * i + h, 1), :] = vd_raw[i, :, 128 * h:128 * h + 128]
    loads[5].wait()
    flat[pl.ds(BASE[5], 24), :] = vf_raw[...]

    with jax.named_scope("enter"):
        pl.semaphore_wait(barrier, 10)

    def d2d(k, i1, i2):
        q1, q2 = ring(ORDER[k][0], FAR[i1]), ring(ORDER[k][1], FAR[i2])
        at = (k, q1, pl.ds(4 * q2, 4))
        return remote(psl.at[at], drx.at[at], dsend.at[k, i1, i2], drecv.at[k, i1, i2], partner)

    for i2 in range(4):
        for i1 in range(4):
            for k in colours:
                q1, q2 = ring(ORDER[k][0], FAR[i1]), ring(ORDER[k][1], FAR[i2])

                def pick(j, k=k, q1=q1, q2=q2):
                    row = SHARD * shard_of(k, q1, q2, j, 1 - core) + PART * k
                    psl[k, q1, 4 * q2 + j] = flat[pl.ds(row, PART), :]
                loop(4, pick, unroll=2)
                d2d(k, i1, i2).start()

    def add_core(k, i1, i2):
        q1, q2 = ring(ORDER[k][0], FAR[i1]), ring(ORDER[k][1], FAR[i2])
        with jax.named_scope(f"d2d{i2}_{i1}_{k}"):
            d2d(k, i1, i2).wait_recv()

        def body(j):
            row = SHARD * shard_of(k, q1, q2, j, core) + PART * k
            work[k, q1, 4 * q2 + j] = flat[pl.ds(row, PART), :] + drx[k, q1, 4 * q2 + j]
        loop(4, body, unroll=2)

    PARTS = ((2, 0, 1), (2, 1, -1), (1, 1, 1), (1, 0, 1), (-1, 0, -1), (-1, 1, -1))

    def chunk1(k, i2, shift, half):
        q1, q2 = ring(ORDER[k][0], shift), ring(ORDER[k][1], FAR[i2])
        return work.at[k, q1, pl.ds(4 * q2 + 2 * half, 2)]

    def chunk2(k, shift, half):
        q1, q2 = ring(ORDER[k][0], 0), ring(ORDER[k][1], shift)
        return work.at[k, q1, pl.ds(4 * q2 + 2 * half, 2)]

    def own3(k, shift):
        q1, q2, q3 = ring(ORDER[k][0], 0), ring(ORDER[k][1], 0), ring(ORDER[k][2], shift)
        return work.at[k, q1, 4 * q2 + q3]

    def rs1(k, i2, part):
        shift, half, way = PARTS[part]
        return remote(chunk1(k, i2, shift, half), r1.at[k, i2, part],
                      s1send.at[k, i2, part], s1recv.at[k, i2, part], neighbour(ORDER[k][0], way))

    def rs2(k, part):
        shift, half, way = PARTS[part]
        return remote(chunk2(k, shift, half), r2.at[k, part],
                      s2send.at[k, part], s2recv.at[k, part], neighbour(ORDER[k][1], way))

    def rs3(k, i3):
        return remote(own3(k, FAR[i3]), r3.at[k, i3],
                      s3send.at[k, i3], s3recv.at[k, i3], neighbour(ORDER[k][2], FAR[i3]))

    def add1(k, i2, shift, half, part):
        with jax.named_scope(f"a{i2}_{part}_{k}"):
            rs1(k, i2, part).wait_recv()
        dst = chunk1(k, i2, shift, half)
        dst[...] = dst[...] + r1[k, i2, part]

    def add2(k, shift, half, part):
        with jax.named_scope(f"b{part}_{k}"):
            rs2(k, part).wait_recv()
        dst = chunk2(k, shift, half)
        dst[...] = dst[...] + r2[k, part]

    def first(i2):
        for k in colours:
            add_core(k, 0, i2)
            rs1(k, i2, 0).start()
            rs1(k, i2, 1).start()
        for k in colours:
            add_core(k, 1, i2)
            rs1(k, i2, 2).start()
            add_core(k, 2, i2)
            rs1(k, i2, 4).start()

    def relay(i2):
        for k in colours:
            add1(k, i2, 1, 0, 0)
            rs1(k, i2, 3).start()
            add1(k, i2, -1, 1, 1)
            rs1(k, i2, 5).start()

    def finish(i2):
        for k in colours:
            add_core(k, 3, i2)
            add1(k, i2, 0, 1, 2)
            add1(k, i2, 0, 0, 4)
            add1(k, i2, 0, 0, 3)
            add1(k, i2, 0, 1, 5)
            if i2 == 0:
                rs2(k, 0).start()
                rs2(k, 1).start()
            if i2 == 1:
                rs2(k, 2).start()
            if i2 == 2:
                rs2(k, 4).start()

    first(0)
    first(1)
    relay(0)
    first(2)
    relay(1)
    finish(0)
    first(3)
    relay(2)
    finish(1)
    relay(3)
    finish(2)
    for k in colours:
        add2(k, 1, 0, 0)
        rs2(k, 3).start()
        add2(k, -1, 1, 1)
        rs2(k, 5).start()
    finish(3)
    for k in colours:
        add2(k, 0, 1, 2)
        add2(k, 0, 0, 4)
        add2(k, 0, 0, 3)
        add2(k, 0, 1, 5)
        for i3 in range(3):
            rs3(k, i3).start()

    for k in colours:
        rows = pl.ds(PART * k, PART)
        grad = own3(k, 0)[...]
        for i3 in range(3):
            with jax.named_scope(f"c{i3}_{k}"):
                rs3(k, i3).wait_recv()
            grad = grad + r3[k, i3]
        grad = grad * (1.0 / 128.0)
        m_new = BETA_ONE * m_ref[rows, :] + (1.0 - BETA_ONE) * grad
        v_new = BETA_TWO * v_ref[rows, :] + (1.0 - BETA_TWO) * grad * grad
        m_hat = m_new / (1.0 - BETA_ONE ** ADAM_STEP)
        v_hat = v_new / (1.0 - BETA_TWO ** ADAM_STEP)
        m_out[rows, :] = m_new
        v_out[rows, :] = v_new
        w_out[rows, :] = w_ref[rows, :] - LEARN_RATE * m_hat / (jnp.sqrt(v_hat) + ADAM_EPS)

    def slot(k, s1, s2, s3):
        axes = ORDER[k]
        return 16 * ring(axes[0], s1) + 4 * ring(axes[1], s2) + ring(axes[2], s3)

    for k in colours:
        own = slot(k, 0, 0, 0)
        if k < 2:
            ag[k, core, own] = w_out[pl.ds(APART * k, APART), :].astype(BF16)
        else:
            vals = jnp.concatenate([w_out[pl.ds(120, 57), :], jnp.zeros((3, 128), F32)], axis=0)
            ag[k, core, own] = vals.astype(BF16)

    def unpack(k, c, s1, s2):
        q1, q2 = ring(ORDER[k][0], s1), ring(ORDER[k][1], s2)
        size = APART if k < 2 else 57

        def body(j):
            row = SHARD * shard_of(k, q1, q2, j, c) + APART * k
            flat[pl.ds(row, size), :] = ag[k, c, 16 * q1 + 4 * q2 + j].astype(F32)[:size]
        loop(4, body, unroll=2)

    NEAR = (0, -1, 1, 2)

    def g2(k, i, came):
        way = (1, -1, 2)[i]
        ref = ag.at[k, core, slot(k, 0, 0, -way if came else 0)]
        return remote(ref, ref, g2send.at[k, i], g2recv.at[k, i], neighbour(ORDER[k][2], way))

    def g1(k, i3, part, came):
        onward = 1 if i3 in (0, 3) else -1
        way = (1, -1, onward)[part]
        start = (0, 0, -onward)[part]
        ref = ag.at[k, core, slot(k, 0, start - way if came else start, NEAR[i3])]
        return remote(ref, ref, g1send.at[k, i3, part], g1recv.at[k, i3, part], neighbour(ORDER[k][1], way))

    def g0(k, i2, part, came):
        way = (1, -1, 1, -1)[part]
        start = (0, 0, -1, 1)[part]
        q1 = ring(ORDER[k][0], start - way if came else start)
        at = 16 * q1 + 4 * ring(ORDER[k][1], NEAR[i2])
        if part >= 2:
            ref = ag.at[k, core, pl.ds(at + 2 * (part - 2), 2)]
        else:
            ref = ag.at[k, core, pl.ds(at, 4)]
        return remote(ref, ref, g0send.at[k, i2, part], g0recv.at[k, i2, part], neighbour(ORDER[k][0], way))

    def share(k, i1, i2, c):
        at = 16 * ring(ORDER[k][0], NEAR[i1]) + 4 * ring(ORDER[k][1], NEAR[i2])
        ref = ag.at[k, c, pl.ds(at, 4)]
        return remote(ref, ref, shsend.at[k, i1, i2], shrecv.at[k, i1, i2], partner)

    def give(k, i1, i2):
        share(k, i1, i2, core).start()

    def take(k, i1, i2):
        with jax.named_scope(f"s{i1}_{i2}_{k}"):
            share(k, i1, i2, 1 - core).wait_recv()
        unpack(k, 1 - core, NEAR[i1], NEAR[i2])

    def got(copy, name):
        with jax.named_scope(name):
            copy.wait_recv()

    def group(k, i2):
        g0(k, i2, 0, False).start()
        g0(k, i2, 1, False).start()
        give(k, 0, i2)

    def onward0(k, i2):
        got(g0(k, i2, 0, True), f"f{i2}_0_{k}")
        g0(k, i2, 2, False).start()
        give(k, 1, i2)
        got(g0(k, i2, 1, True), f"f{i2}_1_{k}")
        g0(k, i2, 3, False).start()
        give(k, 2, i2)

    def last0(k, i2):
        got(g0(k, i2, 2, True), f"f{i2}_2_{k}")
        got(g0(k, i2, 3, True), f"f{i2}_3_{k}")
        give(k, 3, i2)

    for k in colours:
        for i in range(3):
            g2(k, i, False).start()
        g1(k, 0, 0, False).start()
        g1(k, 0, 1, False).start()
    for i in range(3):
        for k in colours:
            got(g2(k, i, True), f"d{i}_{k}")
            g1(k, i + 1, 0, False).start()
            g1(k, i + 1, 1, False).start()
            if i == 2:
                group(k, 0)
    for k in colours:
        unpack(k, core, 0, 0)
    for i3 in range(4):
        for k in colours:
            for part in range(2):
                got(g1(k, i3, part, True), f"e{i3}_{part}_{k}")
                if part == (0 if i3 in (0, 3) else 1):
                    g1(k, i3, 2, False).start()
            if i3 == 3:
                group(k, 1)
                group(k, 2)
    for k in colours:
        onward0(k, 0)
    for k in colours:
        for i3 in range(4):
            got(g1(k, i3, 2, True), f"e{i3}_2_{k}")
        group(k, 3)
    for k in colours:
        for i2 in (1, 2, 3):
            unpack(k, core, 0, NEAR[i2])
    for k in colours:
        take(k, 0, 0)
    for k in colours:
        last0(k, 0)
    for i2 in (1, 2, 3):
        for k in colours:
            onward0(k, i2)
        for k in colours:
            for i1 in (1, 2):
                unpack(k, core, NEAR[i1], NEAR[i2 - 1])
                take(k, i1, i2 - 1)
            take(k, 0, i2)
            unpack(k, core, 2, NEAR[i2 - 1])
            take(k, 3, i2 - 1)
        for k in colours:
            last0(k, i2)
    for k in colours:
        for i1 in (1, 2, 3):
            unpack(k, core, NEAR[i1], NEAR[3])
    for i1 in (1, 2, 3):
        for k in colours:
            take(k, i1, 3)

    for k in colours:
        for i in range(4):
            for j in range(4):
                d2d(k, i, j).wait_send()
                share(k, i, j, core).wait_send()
                g0(k, i, j, False).wait_send()
            for part in range(6):
                rs1(k, i, part).wait_send()
            for part in range(3):
                g1(k, i, part, False).wait_send()
        for part in range(6):
            rs2(k, part).wait_send()
        for part in range(3):
            rs3(k, part).wait_send()
            g2(k, part, False).wait_send()


def apply_kernel(ids, flat, act, m_in, v_in, w_in,
                 emb_out, attn_out, in_out, ff_out, vd_out, vf_out, y_out, m_out, v_out, w_out,
                 emb_v, attn_v, in_v, out_v, vd_v, vf_v, rows_v, sems):
    copies = []

    def send(src, dst):
        copy = pltpu.make_async_copy(src, dst, sems.at[len(copies)])
        copy.start()
        copies.append(copy)

    for src, dst in ((m_in, m_out), (v_in, v_out), (w_in, w_out)):
        send(src, dst)
    stage = (emb_v, attn_v, in_v, out_v)
    outs = (emb_out, attn_out, in_out, ff_out)
    for n in range(4):
        tiles, base, dst = TILES[n], BASE[n], stage[n]

        def pack(g, tiles=tiles, base=base, dst=dst):
            rows = pl.ds(pl.multiple_of(16 * g, 16), 16)
            for c in range(tiles):
                vals = flat[pl.ds(base + g * (16 * tiles) + c, 16, stride=tiles), :]
                dst[rows, 128 * c:128 * c + 128] = vals.astype(BF16)
        loop(GROUPS[n] // 2, pack, unroll=8 // tiles)
        send(dst, outs[n])
    for r in range(9):
        for h in range(2):
            vals = flat[pl.ds(BASE[4] + 2 * r + h, 3, stride=18), :]
            vd_v[r, :, 128 * h:128 * h + 128] = vals.astype(BF16)
    for c in range(8):
        vf_v[:, 128 * c:128 * c + 128] = flat[pl.ds(BASE[5] + c, 3, stride=8), :].astype(BF16)
    send(vd_v, vd_out)
    send(vf_v, vf_out)

    def look(i):
        rows_v[pl.ds(2 * i, 2), :] = flat[pl.ds(2 * ids[i], 2), :]
    loop(256, look, unroll=8)

    def bias(row, count):
        flat_vals = flat[pl.ds(row, count), :].astype(BF16).astype(F32)
        return jnp.concatenate([flat_vals[i:i + 1] for i in range(count)], axis=1)
    emb = jnp.concatenate([rows_v[pl.ds(0, 256, stride=2), :], rows_v[pl.ds(1, 256, stride=2), :]], axis=1)
    hidden = (emb * 16.0 + act[...].astype(F32)).astype(BF16)
    pre = jnp.dot(hidden, in_v[0:256, :], preferred_element_type=F32) + bias(BASE[5], 8)
    inner = jax.nn.gelu(pre, approximate=True).astype(BF16)
    y = jnp.dot(inner, out_v[0:1024, :], preferred_element_type=F32) + bias(BASE[4] + 16, 2)
    y_out[...] = y.astype(BF16)
    for copy in copies:
        copy.wait()


def tiled(grad, width):
    flat = grad.reshape(-1, 8, width // 128, 128)
    return flat.transpose(0, 2, 1, 3)


def solution(mesh):
    def device_step(g_emb, g_attn, g_in, g_out, g_vecd, g_vecf, opt_m, opt_v, master, tok_ids, act_in):
        shapes = [g.shape[1:] for g in (g_emb, g_attn, g_in, g_out, g_vecd, g_vecf)]
        grads = (tiled(g_emb, 256), tiled(g_attn, 256), tiled(g_in, 1024), tiled(g_out, 256),
                 g_vecd.transpose(1, 2, 0, 3).reshape(27, 1, 256), g_vecf.reshape(24, 128))
        state = [s.reshape(SHARD, 128) for s in (opt_m, opt_v, master)]
        anywhere = pl.BlockSpec(memory_space=pltpu.HBM)
        vmem = pl.BlockSpec(memory_space=pltpu.VMEM)
        slots = pltpu.VMEM((3, 4, 16, PART, 128), F32)
        dma = pltpu.SemaphoreType.DMA
        shard = pltpu.VMEM((SHARD, 128), F32)
        m_new, v_new, w_new, flat = pl.pallas_call(
            sync_kernel,
            name="sync",
            out_shape=(shard, shard, shard, pltpu.VMEM((ROWS, 128), F32)),
            in_specs=[anywhere] * 6 + [vmem] * 3,
            out_specs=[vmem] * 4,
            scratch_shapes=[pltpu.VMEM(g.shape, F32) for g in grads] + [
                pltpu.VMEM((3, 2, 64, APART, 128), BF16), slots, slots, slots,
                pltpu.VMEM((3, 4, 6, 2, PART, 128), F32),
                pltpu.VMEM((3, 6, 2, PART, 128), F32),
                pltpu.VMEM((3, 3, PART, 128), F32),
                dma((6,)), dma((3, 4, 4)), dma((3, 4, 4)), dma((3, 4, 6)), dma((3, 4, 6)),
                dma((3, 6)), dma((3, 6)), dma((3, 3)), dma((3, 3)),
                dma((3, 3)), dma((3, 3)), dma((3, 4, 3)), dma((3, 4, 3)),
                dma((3, 4, 4)), dma((3, 4, 4)), dma((3, 4, 4)), dma((3, 4, 4))],
            compiler_params=pltpu.CompilerParams(
                collective_id=0, has_side_effects=True, vmem_limit_bytes=50 * 1048576),
        )(*grads, *state)

        staged = [(2048, 256), (3072, 256), (768, 1024), (3072, 256), (9, 3, 256), (3, 1024)]
        state_out = jax.ShapeDtypeStruct((SHARD, 128), F32)
        outs = pl.pallas_call(
            apply_kernel,
            name="apply",
            out_shape=[jax.ShapeDtypeStruct(s, BF16) for s in staged + [(256, 256)]] + [state_out] * 3,
            in_specs=[pl.BlockSpec(memory_space=pltpu.SMEM)] + [vmem] * 5,
            out_specs=[anywhere] * 6 + [vmem] + [anywhere] * 3,
            scratch_shapes=[pltpu.VMEM(s, BF16) for s in staged] + [
                pltpu.VMEM((512, 128), F32), dma((9,))],
            compiler_params=pltpu.CompilerParams(vmem_limit_bytes=24 * 1048576),
        )(tok_ids, flat, act_in, m_new, v_new, w_new)
        halves = [o.reshape(s) for o, s in zip(outs[:4], shapes)]
        halves += [outs[4].transpose(1, 0, 2), outs[5]]
        return (*[o.reshape(-1) for o in outs[7:]], *halves, outs[6])

    grad_specs = tuple(P(AXES, *([None] * (grad_rank - 1))) for grad_rank in GRAD_RANKS)
    in_specs = grad_specs + (P(AXES), P(AXES), P(AXES), P(AXES), P(AXES, None))
    out_specs = (P(AXES), P(AXES), P(AXES), P(), P(), P(), P(), P(), P(), P(AXES, None))
    return jax.shard_map(device_step, mesh=mesh, in_specs=in_specs, out_specs=out_specs, check_vma=False)
```

time: 83.4 us -> 78 us (0.935)
  Pallas kernels: 82.5 us -> 77.2 us
    pallas_call x1, Pallas kernels: 77.9 us -> 72.6 us  [device_step(): pl.pallas_call(sync_kernel, name='sync', out_shape=(shard, shard, shard,...]
where the time goes in v3:
time: 78 us; the launch traced here: 77.9 us
  Pallas kernels  77.2 us (99%)
    pallas_call x1, Pallas kernels, device_step(): pl.pallas_call(sync_kernel, name='sync', out_shape=(shard, shard, shard,...  72.6 us
    pallas_call x1, Pallas kernels, device_step(): pl.pallas_call(apply_kernel, name='apply', out_shape=[jax.ShapeDtypeStruc...  4.59 us

profile of v3, /device:TPU:1, one launch (start us, length us, event | category | flops | bytes accessed | tf_op | source)
XLA Modules:
  0.0 77.9 jit_solution(6667570851667139666)
XLA Ops:
  0.6 0.0 copy-start
  0.7 0.0 copy-start.1
  0.7 72.6 %sync.1 = (f32[177,128]{1,0:T(8,128)S(1)}, f32[177,128]{1,0:T(8,128)S(1)}, f32[177,128]{1,0:T(8,128)S(1)}, f32[22656,128]{1,0:T(8,128)S(1)}) custom-call(f32[256,2,8,128]{3,2,1,0:T(8,128)} %bitcast.27, f32[384,2,8,128]{3,2,1,0:T(8,128)} %bitcast.24, f32[96,8,8,128]{3,2,1,0:T(8,128)} %bitcast.25, f32[384,2,8,128]{3,2,1,0:T(8,128)} %bitcast.26, ...), custom_call_target="tpu_custom_call" | custom-call | tf_op jit(solution)/shard_map/sync/pallas_call | solution.py:466
  73.3 0.0 copy-done
  73.3 0.0 copy-done.1
  73.3 4.6 %apply.1 = (bf16[2048,256]{1,0:T(8,128)(2,1)}, bf16[3072,256]{1,0:T(8,128)(2,1)}, bf16[768,1024]{1,0:T(8,128)(2,1)}, bf16[3072,256]{1,0:T(8,128)(2,1)}, bf16[9,3...) custom-call(s32[256]{0:T(256)S(1)} %copy-done.1, ...), custom_call_target="tpu_custom_call" | custom-call | tf_op jit(solution)/shard_map/apply/pallas_call | solution.py:487
Async XLA Ops:
  0.6 72.6 %copy-start = (bf16[256,256]{1,0:T(8,128)(2,1)S(1)}, bf16[256,256]{1,0:T(8,128)(2,1)}, u32[]{:S(2)}) copy-start(bf16[256,256]{1,0:T(8,128)(2,1)} %act.1) | copy-start | bytes 393220
  0.7 72.6 %copy-start.1 = (s32[256]{0:T(256)S(1)}, s32[256]{0:T(256)}, u32[]{:S(2)}) copy-start(s32[256]{0:T(256)} %ids.1) | copy-start | bytes 3076

commit v4 on v0

v4 whole, which is shorter than its diff:
```python
import functools
import math
import jax
import jax.numpy as jnp
from jax import lax
from jax.experimental import pallas as pl
from jax.experimental.pallas import tpu as pltpu
from jax.sharding import PartitionSpec as P

LEARN_RATE = 0.002
BETA_ONE = 0.9
BETA_TWO = 0.95
ADAM_EPS = 1e-8
ADAM_STEP = 2
AXES = ("dz", "dy", "dx")
GRAD_RANKS = (3, 5, 4, 4, 4, 3)
MESH = pl.DeviceIdType.MESH

SHARD = 177
RING = 4
LANES = 128
DEVICES = 128
PART = 59
APART = 60
ROWS = 22656
REAL = 22606
BASE = (0, 4096, 10240, 16384, 22528, 22582)
GROUPS = (256, 384, 96, 384)
TILES = (2, 2, 8, 2)
ORDER = ((0, 1, 2), (1, 2, 0), (2, 0, 1))
F32 = jnp.float32
BF16 = jnp.bfloat16


def loop(count, body, unroll=1):
    def step(i, carry):
        body(i)
        return carry
    lax.fori_loop(0, count, step, 0, unroll=unroll)


def shard_of(k, q1, q2, q3, core):
    pos = [None] * 3
    for axis, q in zip(ORDER[k], (q1, q2, q3)):
        pos[axis] = q
    return pos[2] * 32 + pos[1] * 8 + pos[0] * 2 + core


def sync_kernel(e_hbm, a_hbm, i_hbm, o_hbm, vd_hbm, vf_hbm, m_ref, v_ref, w_ref,
                m_out, v_out, w_out, flat,
                e_raw, a_raw, i_raw, o_raw, vd_raw, vf_raw, ag, psl, work, drx,
                r1, r2, r3,
                raw_sem, sent, drecv, s1recv, s2recv, s3recv, g2recv, g1recv, g0recv, shrecv):
    dz, dy, dx = lax.axis_index("dz"), lax.axis_index("dy"), lax.axis_index("dx")
    core = lax.rem(dx, 2)
    pos = (lax.div(dx, 2), dy, dz)
    partner = {"dz": dz, "dy": dy, "dx": dx + 1 - 2 * core}
    colours = range(3)
    FAR = (2, 1, -1, 0)

    def neighbour(axis, shift):
        q = lax.rem(pos[axis] + RING + shift, RING)
        if axis == 0:
            return {"dz": dz, "dy": dy, "dx": q * 2 + core}
        if axis == 1:
            return {"dz": dz, "dy": q, "dx": dx}
        return {"dz": q, "dy": dy, "dx": dx}

    def ring(axis, shift):
        return lax.rem(pos[axis] + RING + shift, RING)

    def remote(src, dst, send_sem, recv_sem, device):
        return pltpu.make_async_remote_copy(
            src_ref=src, dst_ref=dst, send_sem=send_sem, recv_sem=recv_sem,
            device_id=device, device_id_type=MESH)

    def arrive(sem, like, name):
        with jax.named_scope(name):
            pltpu.make_async_copy(like, like, sem).wait()

    def slots_like(count):
        return ag.at[:, 0, pl.ds(0, count)]

    barrier = pltpu.get_barrier_semaphore()
    for axis in range(3):
        for shift in (1, -1, 2):
            pl.semaphore_signal(barrier, inc=1, device_id=neighbour(axis, shift), device_id_type=MESH)
    pl.semaphore_signal(barrier, inc=1, device_id=partner, device_id_type=MESH)

    raws = (e_raw, a_raw, i_raw, o_raw, vd_raw, vf_raw)
    loads = [pltpu.make_async_copy(src, dst, raw_sem.at[n]) for n, (src, dst) in enumerate(
        zip((e_hbm, a_hbm, i_hbm, o_hbm, vd_hbm, vf_hbm), raws))]
    for load in loads:
        load.start()

    flat[pl.ds(REAL, ROWS - REAL), :] = jnp.zeros((ROWS - REAL, LANES), F32)
    for n in range(RING):
        with jax.named_scope(f"load{n}"):
            loads[n].wait()
        tiles, base, raw = TILES[n], BASE[n], raws[n]

        def relayout(g, tiles=tiles, base=base, raw=raw):
            for c in range(tiles):
                flat[pl.ds(base + g * (8 * tiles) + c, 8, stride=tiles), :] = raw[g, c]
        loop(GROUPS[n], relayout, unroll=16 // tiles)
    loads[4].wait()
    for i in range(27):
        for h in range(2):
            flat[pl.ds(BASE[4] + 2 * i + h, 1), :] = vd_raw[i, :, LANES * h:LANES * h + LANES]
    loads[5].wait()
    flat[pl.ds(BASE[5], 24), :] = vf_raw[...]

    with jax.named_scope("enter"):
        pl.semaphore_wait(barrier, 10)

    def d2d(k, i1, i2):
        q1, q2 = ring(ORDER[k][0], FAR[i1]), ring(ORDER[k][1], FAR[i2])
        at = (k, q1, pl.ds(RING * q2, 4))
        return remote(psl.at[at], drx.at[at], sent.at[0], drecv.at[RING * i2 + i1], partner)

    for i2 in range(RING):
        for i1 in range(RING):
            for k in colours:
                q1, q2 = ring(ORDER[k][0], FAR[i1]), ring(ORDER[k][1], FAR[i2])

                def pick(j, k=k, q1=q1, q2=q2):
                    row = SHARD * shard_of(k, q1, q2, j, 1 - core) + PART * k
                    psl[k, q1, RING * q2 + j] = flat[pl.ds(row, PART), :]
                loop(RING, pick, unroll=2)
                d2d(k, i1, i2).start()

    def add_core(i1, i2):
        arrive(drecv.at[RING * i2 + i1], drx.at[:, 0, pl.ds(0, RING)], f"d{i2}_{i1}")
        for k in colours:
            q1, q2 = ring(ORDER[k][0], FAR[i1]), ring(ORDER[k][1], FAR[i2])

            def body(j, k=k, q1=q1, q2=q2):
                row = SHARD * shard_of(k, q1, q2, j, core) + PART * k
                work[k, q1, RING * q2 + j] = flat[pl.ds(row, PART), :] + drx[k, q1, RING * q2 + j]
            loop(RING, body, unroll=2)

    PARTS = ((2, 0, 1), (2, 1, -1), (1, 1, 1), (1, 0, 1), (-1, 0, -1), (-1, 1, -1))

    ADDS = ((1, 0), (-1, 1), (0, 1), (0, 0), (0, 0), (0, 1))

    def chunk(k, s1, s2, half):
        q1, q2 = ring(ORDER[k][0], s1), ring(ORDER[k][1], s2)
        return work.at[k, q1, pl.ds(RING * q2 + 2 * half, 2)]

    def own3(k, shift):
        q1, q2, q3 = ring(ORDER[k][0], 0), ring(ORDER[k][1], 0), ring(ORDER[k][2], shift)
        return work.at[k, q1, RING * q2 + q3]

    def rs1(i2, *parts):
        for k in colours:
            for part in parts:
                shift, half, way = PARTS[part]
                remote(chunk(k, shift, FAR[i2], half), r1.at[k, i2, part],
                       sent.at[1], s1recv.at[6 * i2 + part], neighbour(ORDER[k][0], way)).start()

    def rs2(*parts):
        for k in colours:
            for part in parts:
                shift, half, way = PARTS[part]
                remote(chunk(k, 0, shift, half), r2.at[k, part],
                       sent.at[2], s2recv.at[part], neighbour(ORDER[k][1], way)).start()

    def add1(i2, part):
        arrive(s1recv.at[6 * i2 + part], r1.at[:, i2, part], f"a{i2}_{part}")
        shift, half = ADDS[part]
        for k in colours:
            dst = chunk(k, shift, FAR[i2], half)
            dst[...] = dst[...] + r1[k, i2, part]

    def add2(part):
        arrive(s2recv.at[part], r2.at[:, part], f"b{part}")
        shift, half = ADDS[part]
        for k in colours:
            dst = chunk(k, 0, shift, half)
            dst[...] = dst[...] + r2[k, part]

    def first(i2):
        add_core(0, i2)
        rs1(i2, 0, 1)
        add_core(1, i2)
        rs1(i2, 2)
        add_core(2, i2)
        rs1(i2, 4)

    def relay(i2):
        add1(i2, 0)
        rs1(i2, 3)
        add1(i2, 1)
        rs1(i2, 5)

    def finish(i2):
        add_core(3, i2)
        for part in (2, 4, 3, 5):
            add1(i2, part)

    first(0)
    first(1)
    relay(0)
    first(2)
    relay(1)
    finish(0)
    rs2(0, 1)
    first(3)
    relay(2)
    finish(1)
    rs2(2)
    relay(3)
    finish(2)
    rs2(4)
    add2(0)
    rs2(3)
    add2(1)
    rs2(5)
    finish(3)
    for part in (2, 4, 3, 5):
        add2(part)
    for k in colours:
        for i3 in colours:
            remote(own3(k, FAR[i3]), r3.at[k, i3], sent.at[3], s3recv.at[0],
                   neighbour(ORDER[k][2], FAR[i3])).start()

    arrive(s3recv.at[0], r3, "c")
    for k in colours:
        rows = pl.ds(PART * k, PART)
        grad = own3(k, 0)[...] + r3[k, 0] + r3[k, 1] + r3[k, 2]
        grad = grad * (1.0 / DEVICES)
        m_new = BETA_ONE * m_ref[rows, :] + (1.0 - BETA_ONE) * grad
        v_new = BETA_TWO * v_ref[rows, :] + (1.0 - BETA_TWO) * grad * grad
        m_hat = m_new / (1.0 - BETA_ONE ** ADAM_STEP)
        v_hat = v_new / (1.0 - BETA_TWO ** ADAM_STEP)
        m_out[rows, :] = m_new
        v_out[rows, :] = v_new
        w_out[rows, :] = w_ref[rows, :] - LEARN_RATE * m_hat / (jnp.sqrt(v_hat) + ADAM_EPS)

    def slot(k, s1, s2, s3):
        axes = ORDER[k]
        return 16 * ring(axes[0], s1) + RING * ring(axes[1], s2) + ring(axes[2], s3)

    for k in colours:
        own = slot(k, 0, 0, 0)
        if k < 2:
            ag[k, core, own] = w_out[pl.ds(APART * k, APART), :].astype(BF16)
        else:
            vals = jnp.concatenate([w_out[pl.ds(120, 57), :], jnp.zeros((3, LANES), F32)], axis=0)
            ag[k, core, own] = vals.astype(BF16)

    def unpack(c, i1, i2):
        for k in colours:
            q1, q2 = ring(ORDER[k][0], NEAR[i1]), ring(ORDER[k][1], NEAR[i2])
            size = APART if k < 2 else 57

            def body(j, k=k, q1=q1, q2=q2, size=size):
                row = SHARD * shard_of(k, q1, q2, j, c) + APART * k
                flat[pl.ds(row, size), :] = ag[k, c, 16 * q1 + RING * q2 + j].astype(F32)[:size]
            loop(RING, body, unroll=2)

    NEAR = (0, -1, 1, 2)

    WAYS = (1, -1, 2)

    def g2(i):
        for k in colours:
            ref = ag.at[k, core, slot(k, 0, 0, 0)]
            remote(ref, ref, sent.at[4], g2recv.at[i], neighbour(ORDER[k][2], WAYS[i])).start()

    ONWARD = (1, -1, -1, 1)

    def g1(i3, part):
        way = (*WAYS, ONWARD[i3])[part if part < 2 else 3]
        start = -ONWARD[i3] if part == 2 else 0
        for k in colours:
            ref = ag.at[k, core, slot(k, 0, start, NEAR[i3])]
            remote(ref, ref, sent.at[5], g1recv.at[3 * i3 + part], neighbour(ORDER[k][1], way)).start()

    def got1(i3, part):
        arrive(g1recv.at[3 * i3 + part], slots_like(1), f"e{i3}_{part}")

    def g0(i2, part):
        way = (1, -1)[part % 2]
        start = -way if part > 1 else 0
        for k in colours:
            at = slot(k, start, NEAR[i2], 0) - ring(ORDER[k][2], 0)
            if part > 1:
                ref = ag.at[k, core, pl.ds(at + 2 * (part - 2), 2)]
            else:
                ref = ag.at[k, core, pl.ds(at, RING)]
            remote(ref, ref, sent.at[6], g0recv.at[RING * i2 + part], neighbour(ORDER[k][0], way)).start()

    def got0(i2, part):
        arrive(g0recv.at[RING * i2 + part], slots_like(2 if part > 1 else 4), f"f{i2}_{part}")

    def give(i1, i2):
        for k in colours:
            at = slot(k, NEAR[i1], NEAR[i2], 0) - ring(ORDER[k][2], 0)
            ref = ag.at[k, core, pl.ds(at, RING)]
            remote(ref, ref, sent.at[7], shrecv.at[RING * i1 + i2], partner).start()

    def take(i1, *places):
        for i2 in places:
            arrive(shrecv.at[RING * i1 + i2], slots_like(RING), f"s{i1}_{i2}")
            unpack(1 - core, i1, i2)

    def mine(i1, *places):
        for i2 in places:
            unpack(core, i1, i2)

    def group(i2):
        g0(i2, 0)
        g0(i2, 1)
        give(0, i2)

    def onward0(i2):
        for part in range(2):
            got0(i2, part)
            g0(i2, part + 2)
            give(part + 1, i2)

    def last0(i2):
        got0(i2, 2)
        got0(i2, 3)
        give(3, i2)

    for i in colours:
        g2(i)
    g1(0, 0)
    g1(0, 1)
    for i in colours:
        arrive(g2recv.at[i], slots_like(1), f"h{i}")
        g1(i + 1, 0)
        g1(i + 1, 1)
    group(0)
    mine(0, 0)
    for i3 in range(RING):
        for part in range(2):
            got1(i3, part)
            if WAYS[part] == ONWARD[i3]:
                g1(i3, 2)
    group(1)
    group(2)
    onward0(0)
    for i3 in range(RING):
        got1(i3, 2)
    group(3)
    mine(0, 1, 2, 3)
    take(0, 0)
    onward0(1)
    onward0(2)
    for i1 in (1, 2):
        mine(i1, 0)
    take(0, 1, 2)
    last0(0)
    for i1 in (1, 2):
        mine(i1, 1, 2)
        take(i1, 0)
    mine(3, 0)
    take(0, 3)
    onward0(3)
    last0(1)
    last0(2)
    mine(3, 1, 2)
    for i1 in (1, 2):
        mine(i1, 3)
        take(i1, 1, 2)
    take(3, 0)
    last0(3)
    mine(3, 3)
    take(3, 1, 2)
    for i1 in (1, 2, 3):
        take(i1, 3)

    for n, like in enumerate((psl, r1, r2, r3, slots_like(3), slots_like(12), slots_like(48), slots_like(64))):
        arrive(sent.at[n], like, f"sent{n}")


def apply_kernel(ids, flat, act, m_in, v_in, w_in,
                 emb_out, attn_out, in_out, ff_out, vd_out, vf_out, y_out, m_out, v_out, w_out,
                 emb_v, attn_v, in_v, out_v, vd_v, vf_v, rows_v, sems):
    copies = []

    def send(src, dst):
        copy = pltpu.make_async_copy(src, dst, sems.at[len(copies)])
        copy.start()
        copies.append(copy)

    for src, dst in ((m_in, m_out), (v_in, v_out), (w_in, w_out)):
        send(src, dst)
    stage = (emb_v, attn_v, in_v, out_v)
    outs = (emb_out, attn_out, in_out, ff_out)
    for n in range(RING):
        tiles, base, dst = TILES[n], BASE[n], stage[n]

        def pack(g, tiles=tiles, base=base, dst=dst):
            rows = pl.ds(pl.multiple_of(16 * g, 16), 16)
            for c in range(tiles):
                vals = flat[pl.ds(base + g * (16 * tiles) + c, 16, stride=tiles), :]
                dst[rows, LANES * c:LANES * c + LANES] = vals.astype(BF16)
        loop(GROUPS[n] // 2, pack, unroll=8 // tiles)
        send(dst, outs[n])
    for r in range(9):
        for h in range(2):
            vals = flat[pl.ds(BASE[4] + 2 * r + h, 3, stride=18), :]
            vd_v[r, :, LANES * h:LANES * h + LANES] = vals.astype(BF16)
    for c in range(8):
        vf_v[:, LANES * c:LANES * c + LANES] = flat[pl.ds(BASE[5] + c, 3, stride=8), :].astype(BF16)
    send(vd_v, vd_out)
    send(vf_v, vf_out)

    def look(i):
        rows_v[pl.ds(2 * i, 2), :] = flat[pl.ds(2 * ids[i], 2), :]
    loop(256, look, unroll=8)

    def bias(row, count):
        flat_vals = flat[pl.ds(row, count), :].astype(BF16).astype(F32)
        return jnp.concatenate([flat_vals[i:i + 1] for i in range(count)], axis=1)
    emb = jnp.concatenate([rows_v[pl.ds(0, 256, stride=2), :], rows_v[pl.ds(1, 256, stride=2), :]], axis=1)
    hidden = (emb * 16.0 + act[...].astype(F32)).astype(BF16)
    pre = jnp.dot(hidden, in_v[0:256, :], preferred_element_type=F32) + bias(BASE[5], 8)
    inner = jax.nn.gelu(pre, approximate=True).astype(BF16)
    y = jnp.dot(inner, out_v[0:1024, :], preferred_element_type=F32) + bias(BASE[4] + 16, 2)
    y_out[...] = y.astype(BF16)
    for copy in copies:
        copy.wait()


def tiled(grad, width):
    flat = grad.reshape(-1, 8, width // LANES, LANES)
    return flat.transpose(0, 2, 1, 3)


def solution(mesh):
    def device_step(g_emb, g_attn, g_in, g_out, g_vecd, g_vecf, opt_m, opt_v, master, tok_ids, act_in):
        shapes = [g.shape[1:] for g in (g_emb, g_attn, g_in, g_out, g_vecd, g_vecf)]
        grads = (tiled(g_emb, 256), tiled(g_attn, 256), tiled(g_in, 1024), tiled(g_out, 256),
                 g_vecd.transpose(1, 2, 0, 3).reshape(27, 1, 256), g_vecf.reshape(24, LANES))
        state = [s.reshape(SHARD, LANES) for s in (opt_m, opt_v, master)]
        anywhere = pl.BlockSpec(memory_space=pltpu.HBM)
        vmem = pl.BlockSpec(memory_space=pltpu.VMEM)
        slots = pltpu.VMEM((3, 4, 16, PART, LANES), F32)
        dma = pltpu.SemaphoreType.DMA
        shard = pltpu.VMEM((SHARD, LANES), F32)
        m_new, v_new, w_new, flat = pl.pallas_call(
            sync_kernel,
            name="sync",
            out_shape=(shard, shard, shard, pltpu.VMEM((ROWS, LANES), F32)),
            in_specs=[anywhere] * 6 + [vmem] * 3,
            out_specs=[vmem] * 4,
            scratch_shapes=[pltpu.VMEM(g.shape, F32) for g in grads] + [
                pltpu.VMEM((3, 2, 64, APART, LANES), BF16), slots, slots, slots,
                pltpu.VMEM((3, 4, 6, 2, PART, LANES), F32),
                pltpu.VMEM((3, 6, 2, PART, LANES), F32),
                pltpu.VMEM((3, 3, PART, LANES), F32),
                *[dma((n,)) for n in (6, 8, 16, 24, 6, 1, 3, 12, 16, 16)]],
            compiler_params=pltpu.CompilerParams(
                collective_id=0, has_side_effects=True, vmem_limit_bytes=50 * 1048576),
        )(*grads, *state)

        staged = [(math.prod(s[:-1]), s[-1]) for s in shapes[:4]] + [(9, 3, 256), shapes[5]]
        state_out = jax.ShapeDtypeStruct((SHARD, LANES), F32)
        outs = pl.pallas_call(
            apply_kernel,
            name="apply",
            out_shape=[jax.ShapeDtypeStruct(s, BF16) for s in staged + [(256, 256)]] + [state_out] * 3,
            in_specs=[pl.BlockSpec(memory_space=pltpu.SMEM)] + [vmem] * 5,
            out_specs=[anywhere] * 6 + [vmem] + [anywhere] * 3,
            scratch_shapes=[pltpu.VMEM(s, BF16) for s in staged] + [
                pltpu.VMEM((512, LANES), F32), dma((9,))],
            compiler_params=pltpu.CompilerParams(vmem_limit_bytes=24 * 1048576),
        )(tok_ids, flat, act_in, m_new, v_new, w_new)
        halves = [o.reshape(s) for o, s in zip(outs[:4], shapes)]
        halves += [outs[4].transpose(1, 0, 2), outs[5]]
        return (*[o.reshape(-1) for o in outs[7:]], *halves, outs[6])

    grad_specs = tuple(P(AXES, *([None] * (grad_rank - 1))) for grad_rank in GRAD_RANKS)
    in_specs = grad_specs + (P(AXES), P(AXES), P(AXES), P(AXES), P(AXES, None))
    out_specs = (P(AXES), P(AXES), P(AXES), P(), P(), P(), P(), P(), P(), P(AXES, None))
    return jax.shard_map(device_step, mesh=mesh, in_specs=in_specs, out_specs=out_specs, check_vma=False)
```

time: 365 us -> 66.1 us (0.18)
  waiting for transfers between devices: 241 us -> 0 us
  local copies, waits for them, and re-layouts: 67.7 us -> 0.01 us
  Pallas kernels: 0 us -> 65.2 us
  other arithmetic: 38.9 us -> 0 us
  between operations: 14.2 us -> 0.69 us
    unnamed x3 -> x0, waiting for transfers between devices: 169 us -> none
    all_gather x1 -> x0, waiting for transfers between devices: 72 us -> none  [device_step(): lax.all_gather(w_new.astype(jnp.bfloat16), AXES, axis=0, tiled=True)]
    pallas_call x0 -> x2, Pallas kernels: none -> 65.2 us  [the longest x1 60.6 us: device_step(): pl.pallas_call(sync_kernel, name='sync', out_shape=(shard, shard, shard,...]
    all_gather x1 -> x0, other arithmetic: 36.4 us -> none  [device_step(): lax.all_gather(w_new.astype(jnp.bfloat16), AXES, axis=0, tiled=True)]
    unnamed x38 -> x4, local copies, waits for them, and re-layouts: 33.9 us -> 0.01 us
    slice x10 -> x0, local copies, waits for them, and re-layouts: 11.4 us -> none  [the longest x7 6.18 us: split_flat(): pieces.append(flat_vals[offset:offset + elem_count].reshape(tensor_shape))]
    pad x1 -> x0, local copies, waits for them, and re-layouts: 10 us -> none  [device_step(): local_flat = jnp.pad(local_flat, (0, shard_len * devices - param_count))]
    reshape x6 -> x0, local copies, waits for them, and re-layouts: 9.89 us -> none  [the longest x5 9.89 us: split_flat(): pieces.append(flat_vals[offset:offset + elem_count].reshape(tensor_shape))]
  transfers between devices with their start and end apart: 2 -> 0, of which waited for: 2 -> 0; matrix products, arithmetic and copies ran while one was open for 0% -> 0% of each run, Pallas kernels for 0% -> 0%
where the time goes in v4:
time: 66.1 us; the launch traced here: 65.9 us
  Pallas kernels  65.2 us (99%)
  between operations  0.69 us (1%)
    pallas_call x1, Pallas kernels, device_step(): pl.pallas_call(sync_kernel, name='sync', out_shape=(shard, shard, shard,...  60.6 us
    pallas_call x1, Pallas kernels, device_step(): pl.pallas_call(apply_kernel, name='apply', out_shape=[jax.ShapeDtypeStruc...  4.59 us

profile of v4, /device:TPU:1, one launch (start us, length us, event | category | flops | bytes accessed | tf_op | source)
XLA Modules:
  0.0 65.9 jit_solution(10536984729752302578)
XLA Ops:
  0.6 0.0 copy-start
  0.7 0.0 copy-start.1
  0.7 60.6 %sync.1 = (f32[177,128]{1,0:T(8,128)S(1)}, f32[177,128]{1,0:T(8,128)S(1)}, f32[177,128]{1,0:T(8,128)S(1)}, f32[22656,128]{1,0:T(8,128)S(1)}) custom-call(f32[256,2,8,128]{3,2,1,0:T(8,128)} %bitcast.27, f32[384,2,8,128]{3,2,1,0:T(8,128)} %bitcast.24, f32[96,8,8,128]{3,2,1,0:T(8,128)} %bitcast.25, f32[384,2,8,128]{3,2,1,0:T(8,128)} %bitcast.26, ...), custom_call_target="tpu_custom_call" | custom-call | tf_op jit(solution)/shard_map/sync/pallas_call | solution.py:446
  61.3 0.0 copy-done
  61.3 0.0 copy-done.1
  61.3 4.6 %apply.1 = (bf16[2048,256]{1,0:T(8,128)(2,1)}, bf16[3072,256]{1,0:T(8,128)(2,1)}, bf16[768,1024]{1,0:T(8,128)(2,1)}, bf16[3072,256]{1,0:T(8,128)(2,1)}, bf16[9,3...) custom-call(s32[256]{0:T(256)S(1)} %copy-done.1, ...), custom_call_target="tpu_custom_call" | custom-call | tf_op jit(solution)/shard_map/apply/pallas_call | solution.py:464
Async XLA Ops:
  0.6 60.7 %copy-start = (bf16[256,256]{1,0:T(8,128)(2,1)S(1)}, bf16[256,256]{1,0:T(8,128)(2,1)}, u32[]{:S(2)}) copy-start(bf16[256,256]{1,0:T(8,128)(2,1)} %act.1) | copy-start | bytes 393220
  0.7 60.7 %copy-start.1 = (s32[256]{0:T(256)S(1)}, s32[256]{0:T(256)}, u32[]{:S(2)}) copy-start(s32[256]{0:T(256)} %ids.1) | copy-start | bytes 3076
